TPU v7x, 128 devices: a whole 4x4x4 slice. The times are simulated.
128 devices in a mesh: gx: 4 (over x), gy: 4 (over y_hi, core), gz: 8 (over z, y_lo).
Axes of the slice: x: 4, y: 4 (y_hi: 2, y_lo: 2; y = y_hi * 2 + y_lo), z: 4, core: 2. Of those that a mesh axis runs over, the one named last changes fastest.
Arguments:
- field: bfloat16 [1, 64, 16, 32, 1024], P(None, None, 'gx', 'gy', 'gz'), may hold values from -6 to 6
- kernel_one: bfloat16 [3, 3, 3, 64, 64], replicated, may hold values from -0.15625 to 0.15625
- bias_one: float32 [64], replicated, may hold values from -3 to 3
- kernel_two: bfloat16 [3, 3, 3, 64, 64], replicated, may hold values from -0.15625 to 0.15625
- bias_two: float32 [64], replicated, may hold values from -3 to 3
- kernel_three: bfloat16 [3, 3, 3, 64, 64], replicated, may hold values from -0.15625 to 0.15625
- bias_three: float32 [64], replicated, may hold values from -3 to 3
Outputs:
- latent: bfloat16 [1, 64, 16, 32, 1024], P(None, None, 'gx', 'gy', 'gz')
All inputs are finite; a program needn't handle non-finite values.
Results may differ from a plain program's by a relative error of at most 0.0048.
Values may be sent and summed in bfloat16 or wider, within the bound.
A program may use at most 256 MiB of HBM per device.

v0:
```python
import jax
import jax.numpy as jnp
from jax import lax
from jax.sharding import PartitionSpec as P


def extended(cells, sides, width):
    for axis, dim in sides:
        count = lax.axis_size(axis)
        head = lax.slice_in_dim(cells, 0, width, axis=dim)
        tail = lax.slice_in_dim(cells, cells.shape[dim] - width, cells.shape[dim], axis=dim)
        cells = jnp.concatenate(
            [
                lax.ppermute(tail, axis, [(i, (i + 1) % count) for i in range(count)]),
                cells,
                lax.ppermute(head, axis, [((i + 1) % count, i) for i in range(count)]),
            ],
            axis=dim,
        )
    return cells


def conv_valid(padded, kernel, bias):
    width = padded.shape[2] - 2
    height = padded.shape[3] - 2
    length = padded.shape[4] - 2
    outputs = kernel.shape[3]
    inputs = kernel.shape[4]
    total = None
    for along_x in range(3):
        for along_y in range(3):
            matrix = jnp.transpose(kernel[along_x, along_y], (1, 0, 2)).reshape(outputs, 3 * inputs)
            stacked = jnp.concatenate(
                [
                    padded[
                        :,
                        :,
                        along_x : along_x + width,
                        along_y : along_y + height,
                        along_z : along_z + length,
                    ]
                    for along_z in range(3)
                ],
                axis=1,
            )
            term = jnp.einsum(
                "oc,bcxyz->boxyz", matrix, stacked, preferred_element_type=jnp.float32
            )
            total = term if total is None else total + term
    total = total + bias[None, :, None, None, None]
    return jax.nn.gelu(total, approximate=False).astype(jnp.bfloat16)


def shards(field, kernel_one, bias_one, kernel_two, bias_two, kernel_three, bias_three):
    layers = ((kernel_one, bias_one), (kernel_two, bias_two), (kernel_three, bias_three))
    values = field
    for kernel, bias in layers:
        padded = extended(values, (("gx", 2), ("gy", 3), ("gz", 4)), 1)
        values = conv_valid(padded, kernel, bias)
    return values


def solution(mesh):
    return jax.shard_map(
        shards,
        mesh=mesh,
        in_specs=(P(None, None, "gx", "gy", "gz"), P(), P(), P(), P(), P(), P()),
        out_specs=P(None, None, "gx", "gy", "gz"),
        check_vma=False,
    )
```

profile of v0, /device:TPU:1, one launch (start us, length us, event | category | flops | bytes accessed | tf_op | source)
XLA Modules:
  0.0 127.3 jit_solution(11029236919054398272)
XLA Ops:
  1.4 2.1 %collective-permute-start = (bf16[1,64,1,8,128]{4,1,3,2,0:T(8,128)(2,1)S(1)}, bf16[1,64,1,8,128]{4,1,3,2,0:T(8,128)(2,1)S(1)}, u32[]{:S(2)}, u32[]{:S(2)}) collective-permute-start(bf16[1,64,1,8,128]{4,1,3,2,0:T(8,128)(2,1)S(1)} %get-tuple-element.104), channel_id=1, source_target_pairs={{0,32},{32,64},{64,96},{96,0},{1,33},{33,65},{65,97},{97,1},{2,34}... | collective-permute-start | bytes 393224 | tf_op jit(solution)/shard_map/ppermute | solution.py:14
  3.5 1.3 %collective-permute-start.1 = (bf16[1,64,1,8,128]{4,1,3,2,0:T(8,128)(2,1)S(1)}, bf16[1,64,1,8,128]{4,1,3,2,0:T(8,128)(2,1)S(1)}, u32[]{:S(2)}, u32[]{:S(2)}) collective-permute-start(bf16[1,64,1,8,128]{4,1,3,2,0:T(8,128)(2,1)S(1)} %get-tuple-element.103), channel_id=1, source_target_pairs={{32,0},{64,32},{96,64},{0,96},{33,1},{65,33},{97,65},{1,97},{34,2}... | collective-permute-start | bytes 393224 | tf_op jit(solution)/shard_map/ppermute | solution.py:16
  4.8 2.8 %collective-permute-done = bf16[1,64,1,8,128]{4,1,3,2,0:T(8,128)(2,1)S(1)} collective-permute-done((bf16[1,64,1,8,128]{4,1,3,2,0:T(8,128)(2,1)S(1)}, bf16[1,64,1,8,128]{4,1,3,2,0:T(8,128)(2,1)S(1)}, u32[]{:S(2)}, u32[]{:S(2)}) %collective-permute-start) | collective-permute-done | bytes 131104 | tf_op jit(solution)/shard_map/ppermute | solution.py:14
  7.9 4.7 %collective-permute-start.2 = (bf16[1,64,6,1,128]{4,1,3,2,0:T(8,128)(2,1)S(1)}, bf16[1,64,6,1,128]{4,1,3,2,0:T(8,128)(2,1)S(1)}, u32[]{:S(2)}, u32[]{:S(2)}) collective-permute-start(bf16[1,64,6,1,128]{4,1,3,2,0:T(8,128)(2,1)S(1)} %get-tuple-element.97), channel_id=1, source_target_pairs={{0,8},{8,16},{16,24},{24,0},{1,9},{9,17},{17,25},{25,1},{2,10},{10... | collective-permute-start | bytes 294920 | tf_op jit(solution)/shard_map/ppermute | solution.py:14
  20.6 3.5 %collective-permute-start.5 = (bf16[1,64,6,10,1]{1,2,4,3,0:T(8,128)(2,1)S(1)}, bf16[1,64,6,10,1]{1,2,4,3,0:T(8,128)(2,1)}, u32[]{:S(2)}, u32[]{:S(2)}) collective-permute-start(bf16[1,64,6,10,1]{1,2,4,3,0:T(8,128)(2,1)S(1)} %copy.108), channel_id=1, source_target_pairs={{1,0},{2,1},{3,2},{4,3},{5,4},{6,5},{7,6},{0,7},{9,8},{10,9},{11,1... | collective-permute-start | bytes 23048 | tf_op jit(solution)/shard_map/ppermute | solution.py:16
  24.1 1.4 %fusion.246 = (bf16[1,64,4,8,128]{4,1,3,2,0:T(8,128)(2,1)}, bf16[1,64,4,8,128]{4,1,3,2,0:T(8,128)(2,1)}, bf16[1,64,4,8,128]{4,1,3,2,0:T(8,128)(2,1)}, bf16[1,64,4,8,128]{4,1,3,2,0:T(8,128)(2,1)}) fusion(bf16[1,64,6,8,128]{4,1,3,2,0:T(8,128)(2,1)S(1)} %constant_dynamic-update-slice_fusion, bf16[1,64,6,1,128]{4,1,3,2,0:T(8,128)(2,1)S(1)} %collective-permute-done.2, ...), kind=kLoop, calls=%fused_computation.304 | loop fusion | flops 1048576 | bytes 3080192 | tf_op jit(solution)/shard_map/concatenate | solution.py:12
  27.2 1.8 %maximum_maximum_fusion = (bf16[1,64,6,10,129]{4,1,3,2,0:T(8,128)(2,1)S(1)}, bf16[1,64,6,10,129]{4,1,3,2,0:T(8,128)(2,1)S(1)}) fusion(bf16[1,64,6,1,128]{4,1,3,2,0:T(8,128)(2,1)S(1)} %collective-permute-done.3, bf16[1,64,6,8,128]{4,1,3,2,0:T(8,128)(2,1)S(1)} %constant_dynamic-update-slice_fusion, bf16[1,64,6,1,128]{4,1,3,2,0:T(8,128)(2,1)S(1)} %collective-permute-done.2, ...), kind=kLoop, calls=%fused_computation | loop fusion | flops 7925760 | bytes 2979840 | tf_op jit(solution)/shard_map/concatenate | solution.py:12
  29.1 2.7 %fusion.278 = (bf16[1,64,4,8,128]{4,1,3,2,0:T(8,128)(2,1)S(1)}, bf16[1,64,4,8,128]{4,1,3,2,0:T(8,128)(2,1)S(1)}, bf16[1,64,4,8,128]{4,1,3,2,0:T(8,128)(2,1)S(1)}...) fusion(bf16[1,64,6,10,129]{4,1,3,2,0:T(8,128)(2,1)S(1)} %get-tu, ...), kind=kLoop, calls=%fused_computation.372 | loop fusion | bytes 18874368 | tf_op jit(solution)/shard_map/slice | solution.py:35
  39.4 3.1 %fusion.191 = bf16[1,64,4,8,128]{4,1,3,2,0:T(8,128)(2,1)S(1)} fusion(f32[4,8,128,64]{2,3,1,0:T(8,128)S(1)} %fusion.27, f32[4,8,128,64]{2,3,1,0:T(8,128)S(1)} %fusion.33, f32[4,8,128,64]{2,3,1,0:T(8,128)S(1)} %fusion.39, f32[4,8,128,64]{2,3,1,0:T(8,128)S(1)} %fusion.70, f32[4,8,128,64]{2,3,1,0:T(8,128)S(1)} %fusion.65, f32[4,8,128,64]{2,3,1,0:T(8,128)S(1)} %fusion.60, ...), kind=kOutput, calls=%fused_computation.223 | convolution fusion | flops 124780544 | bytes 10510592 | tf_op jit(solution)/shard_map/oc,bcxyz->boxyz/dot_general | solution.py:46
  43.5 1.7 %collective-permute-start.7 = (bf16[1,64,1,8,128]{4,1,3,2,0:T(8,128)(2,1)S(1)}, bf16[1,64,1,8,128]{4,1,3,2,0:T(8,128)(2,1)S(1)}, u32[]{:S(2)}, u32[]{:S(2)}) collective-permute-start(bf16[1,64,1,8,128]{4,1,3,2,0:T(8,128)(2,1)S(1)} %get-tuple-element.102), channel_id=1, source_target_pairs={{32,0},{64,32},{96,64},{0,96},{33,1},{65,33},{97,65},{1,97},{34,2}... | collective-permute-start | bytes 393224 | tf_op jit(solution)/shard_map/ppermute | solution.py:16
  45.3 2.4 %collective-permute-done.6 = bf16[1,64,1,8,128]{4,1,3,2,0:T(8,128)(2,1)S(1)} collective-permute-done((bf16[1,64,1,8,128]{4,1,3,2,0:T(8,128)(2,1)S(1)}, bf16[1,64,1,8,128]{4,1,3,2,0:T(8,128)(2,1)S(1)}, u32[]{:S(2)}, u32[]{:S(2)}) %collective-permute-start.6) | collective-permute-done | bytes 131104 | tf_op jit(solution)/shard_map/ppermute | solution.py:14
  47.6 5.5 %collective-permute-start.8 = (bf16[1,64,6,1,128]{4,1,3,2,0:T(8,128)(2,1)S(1)}, bf16[1,64,6,1,128]{4,1,3,2,0:T(8,128)(2,1)S(1)}, u32[]{:S(2)}, u32[]{:S(2)}) collective-permute-start(bf16[1,64,6,1,128]{4,1,3,2,0:T(8,128)(2,1)S(1)} %get-tuple-element.93), channel_id=1, source_target_pairs={{0,8},{8,16},{16,24},{24,0},{1,9},{9,17},{17,25},{25,1},{2,10},{10... | collective-permute-start | bytes 294920 | tf_op jit(solution)/shard_map/ppermute | solution.py:14
  61.4 3.0 %collective-permute-start.11 = (bf16[1,64,6,10,1]{1,2,4,3,0:T(8,128)(2,1)S(1)}, bf16[1,64,6,10,1]{1,2,4,3,0:T(8,128)(2,1)}, u32[]{:S(2)}, u32[]{:S(2)}) collective-permute-start(bf16[1,64,6,10,1]{1,2,4,3,0:T(8,128)(2,1)S(1)} %copy.133), channel_id=1, source_target_pairs={{1,0},{2,1},{3,2},{4,3},{5,4},{6,5},{7,6},{0,7},{9,8},{10,9},{11,1... | collective-permute-start | bytes 23048 | tf_op jit(solution)/shard_map/ppermute | solution.py:16
  65.8 1.3 %fusion.285 = (bf16[1,64,4,8,128]{4,1,3,2,0:T(8,128)(2,1)S(1)}, bf16[1,64,4,8,128]{4,1,3,2,0:T(8,128)(2,1)}, bf16[1,64,4,8,128]{4,1,3,2,0:T(8,128)(2,1)}) fusion(bf16[1,64,6,9,128]{4,1,3,2,0:T(8,128)(2,1)S(1)} %get-tuple-element.91), kind=kLoop, calls=%fused_computation.379 | loop fusion | bytes 3145728 | tf_op jit(solution)/shard_map/slice | solution.py:35
  68.9 2.8 %maximum_maximum_fusion.1 = (bf16[1,64,6,10,129]{4,1,3,2,0:T(8,128)(2,1)S(1)}, bf16[1,64,6,10,129]{4,1,3,2,0:T(8,128)(2,1)S(1)}) fusion(bf16[1,64,6,1,128]{4,1,3,2,0:T(8,128)(2,1)S(1)} %collective-permute-done.9, bf16[1,64,1,8,128]{4,1,3,2,0:T(8,128)(2,1)S(1)} %collective-permute-done.7, bf16[1,64,4,8,128]{4,1,3,2,0:T(8,128)(2,1)S(1)} %fusion.191, ...), kind=kLoop, calls=%fused_computation.2 | loop fusion | flops 11888640 | bytes 2979840 | tf_op jit(solution)/shard_map/concatenate | solution.py:12
  72.9 1.4 %fusion.277 = (bf16[1,64,4,8,128]{4,1,3,2,0:T(8,128)(2,1)S(1)}, bf16[1,64,4,8,128]{4,1,3,2,0:T(8,128)(2,1)S(1)}, bf16[1,64,4,8,128]{4,1,3,2,0:T(8,128)(2,1)S(1)}...) fusion(bf16[1,64,6,10,129]{4,1,3,2,0:T(8,128)(2,1)S(1)} %get-tu, ...), kind=kLoop, calls=%fused_computation.371 | loop fusion | bytes 9437184 | tf_op jit(solution)/shard_map/slice | solution.py:35
  81.6 3.0 %fusion.194 = bf16[1,64,4,8,128]{4,1,3,2,0:T(8,128)(2,1)S(1)} fusion(f32[4,8,128,64]{2,3,1,0:T(8,128)S(1)} %fusion.115, f32[4,8,128,64]{2,3,1,0:T(8,128)S(1)} %fusion.15, f32[4,8,128,64]{2,3,1,0:T(8,128)S(1)} %fusion.108, f32[4,8,128,64]{2,3,1,0:T(8,128)S(1)} %fusion.103, f32[4,8,128,64]{2,3,1,0:T(8,128)S(1)} %fusion.98, ...), kind=kOutput, calls=%fused_computation.226 | convolution fusion | flops 124780544 | bytes 10510592 | tf_op jit(solution)/shard_map/oc,bcxyz->boxyz/dot_general | solution.py:46
  85.6 2.1 %collective-permute-start.13 = (bf16[1,64,1,8,128]{4,1,3,2,0:T(8,128)(2,1)S(1)}, bf16[1,64,1,8,128]{4,1,3,2,0:T(8,128)(2,1)S(1)}, u32[]{:S(2)}, u32[]{:S(2)}) collective-permute-start(bf16[1,64,1,8,128]{4,1,3,2,0:T(8,128)(2,1)S(1)} %get-tuple-element.100), channel_id=1, source_target_pairs={{32,0},{64,32},{96,64},{0,96},{33,1},{65,33},{97,65},{1,97},{34,2}... | collective-permute-start | bytes 393224 | tf_op jit(solution)/shard_map/ppermute | solution.py:16
  87.7 2.3 %collective-permute-done.12 = bf16[1,64,1,8,128]{4,1,3,2,0:T(8,128)(2,1)S(1)} collective-permute-done((bf16[1,64,1,8,128]{4,1,3,2,0:T(8,128)(2,1)S(1)}, bf16[1,64,1,8,128]{4,1,3,2,0:T(8,128)(2,1)S(1)}, u32[]{:S(2)}, u32[]{:S(2)}) %collective-permute-start.12) | collective-permute-done | bytes 131104 | tf_op jit(solution)/shard_map/ppermute | solution.py:14
  90.0 4.7 %collective-permute-start.14 = (bf16[1,64,6,1,128]{4,1,3,2,0:T(8,128)(2,1)S(1)}, bf16[1,64,6,1,128]{4,1,3,2,0:T(8,128)(2,1)S(1)}, u32[]{:S(2)}, u32[]{:S(2)}) collective-permute-start(bf16[1,64,6,1,128]{4,1,3,2,0:T(8,128)(2,1)S(1)} %get-tuple-element.89), channel_id=1, source_target_pairs={{0,8},{8,16},{16,24},{24,0},{1,9},{9,17},{17,25},{25,1},{2,10},{10... | collective-permute-start | bytes 294920 | tf_op jit(solution)/shard_map/ppermute | solution.py:14
  102.4 3.6 %collective-permute-start.17 = (bf16[1,64,6,10,1]{1,2,4,3,0:T(8,128)(2,1)S(1)}, bf16[1,64,6,10,1]{1,2,4,3,0:T(8,128)(2,1)}, u32[]{:S(2)}, u32[]{:S(2)}) collective-permute-start(bf16[1,64,6,10,1]{1,2,4,3,0:T(8,128)(2,1)S(1)} %copy.155), channel_id=1, source_target_pairs={{1,0},{2,1},{3,2},{4,3},{5,4},{6,5},{7,6},{0,7},{9,8},{10,9},{11,1... | collective-permute-start | bytes 23048 | tf_op jit(solution)/shard_map/ppermute | solution.py:16
  110.5 2.8 %maximum_maximum_fusion.2 = (bf16[1,64,6,10,129]{4,1,3,2,0:T(8,128)(2,1)S(1)}, bf16[1,64,6,10,129]{4,1,3,2,0:T(8,128)(2,1)S(1)}) fusion(bf16[1,64,6,1,128]{4,1,3,2,0:T(8,128)(2,1)S(1)} %collective-permute-done.15, bf16[1,64,1,8,128]{4,1,3,2,0:T(8,128)(2,1)S(1)} %collective-permute-done.13, bf16[1,64,4,8,128]{4,1,3,2,0:T(8,128)(2,1)S(1)} %fusion.194, ...), kind=kLoop, calls=%fused_computation.4 | loop fusion | flops 11888640 | bytes 2979840 | tf_op jit(solution)/shard_map/concatenate | solution.py:12
  114.5 1.4 %fusion.275 = (bf16[1,64,4,8,128]{4,1,3,2,0:T(8,128)(2,1)S(1)}, bf16[1,64,4,8,128]{4,1,3,2,0:T(8,128)(2,1)S(1)}, bf16[1,64,4,8,128]{4,1,3,2,0:T(8,128)(2,1)S(1)}...) fusion(bf16[1,64,6,10,129]{4,1,3,2,0:T(8,128)(2,1)S(1)} %get-tu, ...), kind=kLoop, calls=%fused_computation.369 | loop fusion | bytes 9437184 | tf_op jit(solution)/shard_map/slice | solution.py:35
  123.2 3.0 %fusion.197 = bf16[1,64,4,8,128]{4,1,3,2,0:T(8,128)(2,1)S(1)} fusion(f32[4,8,128,64]{2,3,1,0:T(8,128)S(1)} %fusion.154, f32[4,8,128,64]{2,3,1,0:T(8,128)S(1)} %fusion.3, f32[4,8,128,64]{2,3,1,0:T(8,128)S(1)} %fusion.147, f32[4,8,128,64]{2,3,1,0:T(8,128)S(1)} %fusion.142, f32[4,8,128,64]{2,3,1,0:T(8,128)S(1)} %fusion.137, ...), kind=kOutput, calls=%fused_computation.229 | convolution fusion | flops 124780544 | bytes 10510592 | tf_op jit(solution)/shard_map/oc,bcxyz->boxyz/dot_general | solution.py:46
  (211 shorter events, 62.2 us)
Async XLA Ops:
  0.0 7.6 %copy-start = (bf16[1,64,4,8,128]{4,3,2,1,0:T(8,128)(2,1)S(1)}, bf16[1,64,4,8,128]{4,3,2,1,0:T(8,128)(2,1)}, u32[]{:S(2)}) copy-start(bf16[1,64,4,8,128]{4,3,2,1,0:T(8,128)(2,1)} %param.7) | copy-start | bytes 1572868
  0.0 12.6 %copy-start.15 = (bf16[3,3,3,64,64]{4,3,2,1,0:T(8,128)(2,1)S(1)}, bf16[3,3,3,64,64]{4,3,2,1,0:T(8,128)(2,1)}, u32[]{:S(2)}) copy-start(bf16[3,3,3,64,64]{4,3,2,1,0:T(8,128)(2,1)} %param.8) | copy-start | bytes 663556
  1.4 6.2 %collective-permute-start = (bf16[1,64,1,8,128]{4,1,3,2,0:T(8,128)(2,1)S(1)}, bf16[1,64,1,8,128]{4,1,3,2,0:T(8,128)(2,1)S(1)}, u32[]{:S(2)}, u32[]{:S(2)}) collective-permute-start(bf16[1,64,1,8,128]{4,1,3,2,0:T(8,128)(2,1)S(1)} %get-tuple-element.104), channel_id=1, source_target_pairs={{0,32},{32,64},{64,96},{96,0},{1,33},{33,65},{65,97},{97,1},{2,34}... | collective-permute-start | bytes 393224 | tf_op jit(solution)/shard_map/ppermute | solution.py:14
  3.5 4.4 %collective-permute-start.1 = (bf16[1,64,1,8,128]{4,1,3,2,0:T(8,128)(2,1)S(1)}, bf16[1,64,1,8,128]{4,1,3,2,0:T(8,128)(2,1)S(1)}, u32[]{:S(2)}, u32[]{:S(2)}) collective-permute-start(bf16[1,64,1,8,128]{4,1,3,2,0:T(8,128)(2,1)S(1)} %get-tuple-element.103), channel_id=1, source_target_pairs={{32,0},{64,32},{96,64},{0,96},{33,1},{65,33},{97,65},{1,97},{34,2}... | collective-permute-start | bytes 393224 | tf_op jit(solution)/shard_map/ppermute | solution.py:16
  7.6 5.0 %copy-start.20 = (bf16[1,64,1,8,128]{4,1,3,2,0:T(8,128)(2,1)}, bf16[1,64,1,8,128]{4,1,3,2,0:T(8,128)(2,1)S(1)}, u32[]{:S(2)}) copy-start(bf16[1,64,1,8,128]{4,1,3,2,0:T(8,128)(2,1)S(1)} %collective-permute-done) | copy-start | bytes 393220
  7.8 4.7 %copy-start.18 = (bf16[1,64,1,8,128]{4,1,3,2,0:T(8,128)(2,1)}, bf16[1,64,1,8,128]{4,1,3,2,0:T(8,128)(2,1)S(1)}, u32[]{:S(2)}) copy-start(bf16[1,64,1,8,128]{4,1,3,2,0:T(8,128)(2,1)S(1)} %collective-permute-done.1) | copy-start | bytes 393220
  7.9 10.5 %collective-permute-start.2 = (bf16[1,64,6,1,128]{4,1,3,2,0:T(8,128)(2,1)S(1)}, bf16[1,64,6,1,128]{4,1,3,2,0:T(8,128)(2,1)S(1)}, u32[]{:S(2)}, u32[]{:S(2)}) collective-permute-start(bf16[1,64,6,1,128]{4,1,3,2,0:T(8,128)(2,1)S(1)} %get-tuple-element.97), channel_id=1, source_target_pairs={{0,8},{8,16},{16,24},{24,0},{1,9},{9,17},{17,25},{25,1},{2,10},{10... | collective-permute-start | bytes 294920 | tf_op jit(solution)/shard_map/ppermute | solution.py:14
  12.6 5.8 %collective-permute-start.3 = (bf16[1,64,6,1,128]{4,1,3,2,0:T(8,128)(2,1)S(1)}, bf16[1,64,6,1,128]{4,1,3,2,0:T(8,128)(2,1)S(1)}, u32[]{:S(2)}, u32[]{:S(2)}) collective-permute-start(bf16[1,64,6,1,128]{4,1,3,2,0:T(8,128)(2,1)S(1)} %get-tuple-element.98), channel_id=1, source_target_pairs={{8,0},{16,8},{24,16},{0,24},{9,1},{17,9},{25,17},{1,25},{10,2},{18... | collective-permute-start | bytes 294920 | tf_op jit(solution)/shard_map/ppermute | solution.py:16
  19.6 5.9 %collective-permute-start.4 = (bf16[1,64,6,10,1]{1,2,4,3,0:T(8,128)(2,1)S(1)}, bf16[1,64,6,10,1]{1,2,4,3,0:T(8,128)(2,1)S(1)}, u32[]{:S(2)}, u32[]{:S(2)}) collective-permute-start(bf16[1,64,6,10,1]{1,2,4,3,0:T(8,128)(2,1)S(1)} %copy.106), channel_id=1, source_target_pairs={{0,1},{1,2},{2,3},{3,4},{4,5},{5,6},{6,7},{7,0},{8,9},{9,10},{10,1... | collective-permute-start | bytes 23048 | tf_op jit(solution)/shard_map/ppermute | solution.py:14
  20.6 5.4 %collective-permute-start.5 = (bf16[1,64,6,10,1]{1,2,4,3,0:T(8,128)(2,1)S(1)}, bf16[1,64,6,10,1]{1,2,4,3,0:T(8,128)(2,1)}, u32[]{:S(2)}, u32[]{:S(2)}) collective-permute-start(bf16[1,64,6,10,1]{1,2,4,3,0:T(8,128)(2,1)S(1)} %copy.108), channel_id=1, source_target_pairs={{1,0},{2,1},{3,2},{4,3},{5,4},{6,5},{7,6},{0,7},{9,8},{10,9},{11,1... | collective-permute-start | bytes 23048 | tf_op jit(solution)/shard_map/ppermute | solution.py:16
  39.4 13.8 %copy-start.16 = (bf16[3,3,3,64,64]{4,3,2,1,0:T(8,128)(2,1)S(1)}, bf16[3,3,3,64,64]{4,3,2,1,0:T(8,128)(2,1)}, u32[]{:S(2)}) copy-start(bf16[3,3,3,64,64]{4,3,2,1,0:T(8,128)(2,1)} %param.10) | copy-start | bytes 663556
  42.5 5.1 %collective-permute-start.6 = (bf16[1,64,1,8,128]{4,1,3,2,0:T(8,128)(2,1)S(1)}, bf16[1,64,1,8,128]{4,1,3,2,0:T(8,128)(2,1)S(1)}, u32[]{:S(2)}, u32[]{:S(2)}) collective-permute-start(bf16[1,64,1,8,128]{4,1,3,2,0:T(8,128)(2,1)S(1)} %get-tuple-element.101), channel_id=1, source_target_pairs={{0,32},{32,64},{64,96},{96,0},{1,33},{33,65},{65,97},{97,1},{2,34}... | collective-permute-start | bytes 393224 | tf_op jit(solution)/shard_map/ppermute | solution.py:14
  43.5 4.1 %collective-permute-start.7 = (bf16[1,64,1,8,128]{4,1,3,2,0:T(8,128)(2,1)S(1)}, bf16[1,64,1,8,128]{4,1,3,2,0:T(8,128)(2,1)S(1)}, u32[]{:S(2)}, u32[]{:S(2)}) collective-permute-start(bf16[1,64,1,8,128]{4,1,3,2,0:T(8,128)(2,1)S(1)} %get-tuple-element.102), channel_id=1, source_target_pairs={{32,0},{64,32},{96,64},{0,96},{33,1},{65,33},{97,65},{1,97},{34,2}... | collective-permute-start | bytes 393224 | tf_op jit(solution)/shard_map/ppermute | solution.py:16
  47.6 11.3 %collective-permute-start.8 = (bf16[1,64,6,1,128]{4,1,3,2,0:T(8,128)(2,1)S(1)}, bf16[1,64,6,1,128]{4,1,3,2,0:T(8,128)(2,1)S(1)}, u32[]{:S(2)}, u32[]{:S(2)}) collective-permute-start(bf16[1,64,6,1,128]{4,1,3,2,0:T(8,128)(2,1)S(1)} %get-tuple-element.93), channel_id=1, source_target_pairs={{0,8},{8,16},{16,24},{24,0},{1,9},{9,17},{17,25},{25,1},{2,10},{10... | collective-permute-start | bytes 294920 | tf_op jit(solution)/shard_map/ppermute | solution.py:14
  53.2 5.8 %collective-permute-start.9 = (bf16[1,64,6,1,128]{4,1,3,2,0:T(8,128)(2,1)S(1)}, bf16[1,64,6,1,128]{4,1,3,2,0:T(8,128)(2,1)S(1)}, u32[]{:S(2)}, u32[]{:S(2)}) collective-permute-start(bf16[1,64,6,1,128]{4,1,3,2,0:T(8,128)(2,1)S(1)} %get-tuple-element.94), channel_id=1, source_target_pairs={{8,0},{16,8},{24,16},{0,24},{9,1},{17,9},{25,17},{1,25},{10,2},{18... | collective-permute-start | bytes 294920 | tf_op jit(solution)/shard_map/ppermute | solution.py:16
  60.2 7.0 %collective-permute-start.10 = (bf16[1,64,6,10,1]{1,2,4,3,0:T(8,128)(2,1)S(1)}, bf16[1,64,6,10,1]{1,2,4,3,0:T(8,128)(2,1)S(1)}, u32[]{:S(2)}, u32[]{:S(2)}) collective-permute-start(bf16[1,64,6,10,1]{1,2,4,3,0:T(8,128)(2,1)S(1)} %copy.131), channel_id=1, source_target_pairs={{0,1},{1,2},{2,3},{3,4},{4,5},{5,6},{6,7},{7,0},{8,9},{9,10},{10,1... | collective-permute-start | bytes 23048 | tf_op jit(solution)/shard_map/ppermute | solution.py:14
  61.4 6.2 %collective-permute-start.11 = (bf16[1,64,6,10,1]{1,2,4,3,0:T(8,128)(2,1)S(1)}, bf16[1,64,6,10,1]{1,2,4,3,0:T(8,128)(2,1)}, u32[]{:S(2)}, u32[]{:S(2)}) collective-permute-start(bf16[1,64,6,10,1]{1,2,4,3,0:T(8,128)(2,1)S(1)} %copy.133), channel_id=1, source_target_pairs={{1,0},{2,1},{3,2},{4,3},{5,4},{6,5},{7,6},{0,7},{9,8},{10,9},{11,1... | collective-permute-start | bytes 23048 | tf_op jit(solution)/shard_map/ppermute | solution.py:16
  81.6 13.2 %copy-start.17 = (bf16[3,3,3,64,64]{4,3,2,1,0:T(8,128)(2,1)S(1)}, bf16[3,3,3,64,64]{4,3,2,1,0:T(8,128)(2,1)}, u32[]{:S(2)}) copy-start(bf16[3,3,3,64,64]{4,3,2,1,0:T(8,128)(2,1)} %param.12) | copy-start | bytes 663556
  84.6 5.4 %collective-permute-start.12 = (bf16[1,64,1,8,128]{4,1,3,2,0:T(8,128)(2,1)S(1)}, bf16[1,64,1,8,128]{4,1,3,2,0:T(8,128)(2,1)S(1)}, u32[]{:S(2)}, u32[]{:S(2)}) collective-permute-start(bf16[1,64,1,8,128]{4,1,3,2,0:T(8,128)(2,1)S(1)} %get-tuple-element.99), channel_id=1, source_target_pairs={{0,32},{32,64},{64,96},{96,0},{1,33},{33,65},{65,97},{97,1},{2,34}... | collective-permute-start | bytes 393224 | tf_op jit(solution)/shard_map/ppermute | solution.py:14
  85.6 4.4 %collective-permute-start.13 = (bf16[1,64,1,8,128]{4,1,3,2,0:T(8,128)(2,1)S(1)}, bf16[1,64,1,8,128]{4,1,3,2,0:T(8,128)(2,1)S(1)}, u32[]{:S(2)}, u32[]{:S(2)}) collective-permute-start(bf16[1,64,1,8,128]{4,1,3,2,0:T(8,128)(2,1)S(1)} %get-tuple-element.100), channel_id=1, source_target_pairs={{32,0},{64,32},{96,64},{0,96},{33,1},{65,33},{97,65},{1,97},{34,2}... | collective-permute-start | bytes 393224 | tf_op jit(solution)/shard_map/ppermute | solution.py:16
  90.0 10.6 %collective-permute-start.14 = (bf16[1,64,6,1,128]{4,1,3,2,0:T(8,128)(2,1)S(1)}, bf16[1,64,6,1,128]{4,1,3,2,0:T(8,128)(2,1)S(1)}, u32[]{:S(2)}, u32[]{:S(2)}) collective-permute-start(bf16[1,64,6,1,128]{4,1,3,2,0:T(8,128)(2,1)S(1)} %get-tuple-element.89), channel_id=1, source_target_pairs={{0,8},{8,16},{16,24},{24,0},{1,9},{9,17},{17,25},{25,1},{2,10},{10... | collective-permute-start | bytes 294920 | tf_op jit(solution)/shard_map/ppermute | solution.py:14
  94.8 5.8 %collective-permute-start.15 = (bf16[1,64,6,1,128]{4,1,3,2,0:T(8,128)(2,1)S(1)}, bf16[1,64,6,1,128]{4,1,3,2,0:T(8,128)(2,1)S(1)}, u32[]{:S(2)}, u32[]{:S(2)}) collective-permute-start(bf16[1,64,6,1,128]{4,1,3,2,0:T(8,128)(2,1)S(1)} %get-tuple-element.90), channel_id=1, source_target_pairs={{8,0},{16,8},{24,16},{0,24},{9,1},{17,9},{25,17},{1,25},{10,2},{18... | collective-permute-start | bytes 294920 | tf_op jit(solution)/shard_map/ppermute | solution.py:16
  101.8 7.0 %collective-permute-start.16 = (bf16[1,64,6,10,1]{1,2,4,3,0:T(8,128)(2,1)S(1)}, bf16[1,64,6,10,1]{1,2,4,3,0:T(8,128)(2,1)S(1)}, u32[]{:S(2)}, u32[]{:S(2)}) collective-permute-start(bf16[1,64,6,10,1]{1,2,4,3,0:T(8,128)(2,1)S(1)} %copy.153), channel_id=1, source_target_pairs={{0,1},{1,2},{2,3},{3,4},{4,5},{5,6},{6,7},{7,0},{8,9},{9,10},{10,1... | collective-permute-start | bytes 23048 | tf_op jit(solution)/shard_map/ppermute | solution.py:14
  102.4 6.8 %collective-permute-start.17 = (bf16[1,64,6,10,1]{1,2,4,3,0:T(8,128)(2,1)S(1)}, bf16[1,64,6,10,1]{1,2,4,3,0:T(8,128)(2,1)}, u32[]{:S(2)}, u32[]{:S(2)}) collective-permute-start(bf16[1,64,6,10,1]{1,2,4,3,0:T(8,128)(2,1)S(1)} %copy.155), channel_id=1, source_target_pairs={{1,0},{2,1},{3,2},{4,3},{5,4},{6,5},{7,6},{0,7},{9,8},{10,9},{11,1... | collective-permute-start | bytes 23048 | tf_op jit(solution)/shard_map/ppermute | solution.py:16
  (43 other events, 44.8 us)
where the time goes:
time: 129 us; the launch traced here: 127 us
  local copies, waits for them, and re-layouts  53 us (41%)
  starting transfers between devices  35.5 us (28%)
  matrix products  21.2 us (16%)
  other arithmetic  9.56 us (7%)
  waiting for transfers between devices  7.42 us (6%)
    dot_general x27, matrix products, conv_valid(): jnp.einsum('oc,bcxyz->boxyz', matrix, stacked, preferred_element_type=jnp...  21.2 us
    ppermute x9, starting transfers between devices, extended(): lax.ppermute(tail, axis, [(i, (i + 1) % count) for i in range(count)])  20.2 us
    transpose x30, local copies, waits for them, and re-layouts, conv_valid(): jnp.transpose(kernel[along_x, along_y], (1, 0, 2))  17.4 us
    ppermute x9, starting transfers between devices, extended(): lax.ppermute(head, axis, [((i + 1) % count, i) for i in range(count)])  15.4 us
    slice x9, local copies, waits for them, and re-layouts, conv_valid(): padded[:, :, along_x:along_x + width, along_y:along_y + height, along_z:a...  13.1 us
    unnamed x101, local copies, waits for them, and re-layouts  11.4 us
    concatenate x9, other arithmetic, extended(): jnp.concatenate([lax.ppermute(tail, axis, [(i, (i + 1) % count) for i in...  9.51 us
    ppermute x9, waiting for transfers between devices, extended(): lax.ppermute(tail, axis, [(i, (i + 1) % count) for i in range(count)])  7.4 us
  transfers between devices with their start and end apart: 18, of which 3 were waited for; matrix products, arithmetic and copies ran while one was open for 22% of the time, Pallas kernels for 0%

commit v1 on v0

v1 whole, which is shorter than its diff:
```python
import functools

import jax
import jax.numpy as jnp
from jax import lax
from jax.experimental import pallas as pl
from jax.experimental.pallas import tpu as pltpu
from jax.sharding import PartitionSpec as P

MESH = pl.DeviceIdType.MESH
AXES = ("gx", "gy", "gz")
HALF = 64
LX, LY, LP = 4, 8, 64
FLAT = [(dx, dy, 0) for dx in (-1, 0, 1) for dy in (-1, 0, 1) if (dx, dy) != (0, 0)]
SIDES = [(dx, dy, dz) for dz in (-1, 1) for dx in (-1, 0, 1) for dy in (-1, 0, 1)]
WAYS = FLAT + SIDES


def neighbour(way):
    ids = []
    for axis, step in zip(AXES, way):
        count = lax.axis_size(axis)
        ids.append(lax.rem(lax.axis_index(axis) + step + count, count))
    return tuple(ids)


def message(layer, way, a, zs, zr, send, recv):
    dx, dy, dz = way
    which = WAYS.index(way)
    if dz == 0:
        near_x = {1: LX, -1: 1, 0: pl.ds(1, LX)}[dx]
        far_x = {1: 0, -1: LX + 1, 0: pl.ds(1, LX)}[dx]
        near_y = {1: LY, -1: 1, 0: pl.ds(1, LY)}[dy]
        far_y = {1: 0, -1: LY + 1, 0: pl.ds(1, LY)}[dy]
        source = a.at[layer, near_x, near_y]
        target = a.at[layer, far_x, far_y]
    else:
        side, other = (1, 0) if dz == 1 else (0, 1)
        source = zs.at[layer, side]
        target = zr.at[layer, other, 1 - dx, 1 - dy]
        if dx != 0:
            plane = LX - 1 if dx == 1 else 0
            source = source.at[plane]
            target = target.at[plane]
    return pltpu.make_async_remote_copy(
        src_ref=source,
        dst_ref=target,
        send_sem=send.at[layer, which],
        recv_sem=recv.at[layer, which],
        device_id=neighbour(way),
        device_id_type=MESH,
    )


def kernel(field, weights, bias, out, a, b, zs, zr, edge, halo, send, recv, local):
    load = pltpu.make_async_copy(field, a.at[0, pl.ds(1, LX), pl.ds(1, LY)], local)
    load.start()
    barrier = pltpu.get_barrier_semaphore()
    for way in WAYS:
        pl.semaphore_signal(barrier, inc=1, device_id=neighbour(way), device_id_type=MESH)
    load.wait()

    lane = lax.broadcasted_iota(jnp.int32, (LP, 2 * HALF), 1)
    row = lax.broadcasted_iota(jnp.int32, (LP, 2 * HALF), 0)
    even = lane < HALF
    ends = (even & (row == LP - 1)) | (~even & (row == 0))
    even_row = lax.broadcasted_iota(jnp.int32, (LY, 2 * HALF), 1) < HALF

    def pack_edges(layer):
        for side in range(2):
            for x in range(LX):
                zs[layer, side, x] = edge[side, x].astype(jnp.bfloat16)

    def first_edges(i, carry):
        x, y = i // LY, i % LY
        slab = a[0, x + 1, y + 1].astype(jnp.float32)
        edge[0, x, pl.ds(y, 1), :] = slab[0:1]
        edge[1, x, pl.ds(y, 1), :] = slab[LP - 1 :]
        return carry

    lax.fori_loop(0, LX * LY, first_edges, 0)
    pack_edges(0)
    pl.semaphore_wait(barrier, len(WAYS))

    def copies(layer):
        return [message(layer, way, a, zs, zr, send, recv) for way in WAYS]

    for copy in copies(0):
        copy.start()

    for layer in range(3):
        for copy in copies(layer):
            copy.wait_recv()

        for x in range(LX + 2):
            ix = 0 if x == 0 else 2 if x == LX + 1 else 1
            sx = (x - 1) % LX
            for iy in range(3):
                rows = jnp.where(
                    even_row,
                    zr[layer, 1, ix, iy, sx].astype(jnp.float32),
                    zr[layer, 0, ix, iy, sx].astype(jnp.float32),
                )
                if iy == 0:
                    halo[x, 7:8, :] = rows[7:8]
                elif iy == 1:
                    halo[x, 8:16, :] = rows
                else:
                    halo[x, 16:17, :] = rows[0:1]

        def shift(i, carry):
            x, y = i // (LY + 2), i % (LY + 2)
            slab = a[layer, x, y].astype(jnp.float32)
            up = pltpu.roll(slab, LP - 1, 0)
            down = pltpu.roll(slab, 1, 0)
            fill = jnp.broadcast_to(halo[x, pl.ds(y + 7, 1), :], (LP, 2 * HALF))
            b[x, y] = jnp.where(ends, fill, jnp.where(even, up, down)).astype(jnp.bfloat16)
            return carry

        lax.fori_loop(0, (LX + 2) * (LY + 2), shift, 0)

        def plane(x):
            total = None
            for along_x in range(3):
                for t in range(4):
                    left = jnp.concatenate([a[layer, x + along_x, t + 2 * j] for j in range(LY // 2)], axis=0)
                    right = jnp.concatenate([b[x + along_x, t + 2 * j] for j in range(LY // 2)], axis=0)
                    term = jnp.dot(
                        jnp.concatenate([left, right], axis=1),
                        jnp.concatenate([weights[layer, along_x, t + 1], weights[layer, along_x, t]], axis=1),
                        preferred_element_type=jnp.float32,
                    )
                    total = term if total is None else total + term
            total = total + bias[layer]
            value = 0.5 * total * (1.0 + lax.erf(total * 0.7071067811865476))
            for j in range(LY // 2):
                for side in range(2):
                    y = 2 * j + side
                    slab = value[j * LP : (j + 1) * LP, side * 2 * HALF : (side + 1) * 2 * HALF]
                    if layer < 2:
                        a[layer + 1, x + 1, y + 1] = slab.astype(jnp.bfloat16)
                        edge[0, x, y : y + 1, :] = slab[0:1]
                        edge[1, x, y : y + 1, :] = slab[LP - 1 :]
                    else:
                        out[x, y] = slab.astype(jnp.bfloat16)

        def outer(i, carry):
            plane(i * (LX - 1))
            return carry

        def inner(i, carry):
            plane(i + 1)
            return carry

        lax.fori_loop(0, 2, outer, 0)
        if layer < 2:
            for side in range(2):
                for x in (0, LX - 1):
                    zs[layer + 1, side, x] = edge[side, x].astype(jnp.bfloat16)
            for way in WAYS:
                if way[0] != 0:
                    message(layer + 1, way, a, zs, zr, send, recv).start()
        lax.fori_loop(0, 2, inner, 0)
        if layer < 2:
            for side in range(2):
                for x in range(1, LX - 1):
                    zs[layer + 1, side, x] = edge[side, x].astype(jnp.bfloat16)
            for way in WAYS:
                if way[0] == 0:
                    message(layer + 1, way, a, zs, zr, send, recv).start()

    for layer in range(3):
        for copy in copies(layer):
            copy.wait_send()


def toeplitz(weight):
    taps = jnp.transpose(weight, (0, 1, 2, 4, 3))
    zero = jnp.zeros_like(taps[:, :, 0])
    first, middle, last = taps[:, :, 0], taps[:, :, 1], taps[:, :, 2]
    lower = jnp.concatenate([middle, last, zero, first], axis=2)
    upper = jnp.concatenate([first, middle, last, zero], axis=2)
    block = jnp.concatenate([lower, upper], axis=3)
    return jnp.pad(block, ((0, 0), (1, 1), (0, 0), (0, 0)))


def shards(field, kernel_one, bias_one, kernel_two, bias_two, kernel_three, bias_three):
    channels = field.shape[1]
    cells = field.reshape(channels, LX, LY, LP, 2)
    cells = jnp.transpose(cells, (1, 2, 3, 4, 0)).reshape(LX, LY, LP, 2 * channels)
    weights = jnp.stack([toeplitz(k) for k in (kernel_one, kernel_two, kernel_three)])
    bias = jnp.stack([jnp.tile(v, 4)[None] for v in (bias_one, bias_two, bias_three)])
    vmem = pl.BlockSpec(memory_space=pltpu.VMEM)
    result = pl.pallas_call(
        kernel,
        out_shape=jax.ShapeDtypeStruct((LX, LY, LP, 2 * HALF), jnp.bfloat16),
        in_specs=[pl.BlockSpec(memory_space=pl.ANY), vmem, vmem],
        out_specs=vmem,
        scratch_shapes=[
            pltpu.VMEM((3, LX + 2, LY + 2, LP, 2 * HALF), jnp.bfloat16),
            pltpu.VMEM((LX + 2, LY + 2, LP, 2 * HALF), jnp.bfloat16),
            pltpu.VMEM((3, 2, LX, LY, 2 * HALF), jnp.bfloat16),
            pltpu.VMEM((3, 2, 3, 3, LX, LY, 2 * HALF), jnp.bfloat16),
            pltpu.VMEM((2, LX, LY, 2 * HALF), jnp.float32),
            pltpu.VMEM((LX + 2, 24, 2 * HALF), jnp.float32),
            pltpu.SemaphoreType.DMA((3, len(WAYS))),
            pltpu.SemaphoreType.DMA((3, len(WAYS))),
            pltpu.SemaphoreType.DMA,
        ],
        compiler_params=pltpu.CompilerParams(
            collective_id=0, has_side_effects=True, vmem_limit_bytes=48 * 1024 * 1024
        ),
    )(cells, weights, bias)
    result = result.reshape(LX, LY, LP, 2, channels)
    return jnp.transpose(result, (4, 0, 1, 2, 3)).reshape(1, channels, LX, LY, 2 * LP)


def solution(mesh):
    return jax.shard_map(
        shards,
        mesh=mesh,
        in_specs=(P(None, None, "gx", "gy", "gz"), P(), P(), P(), P(), P(), P()),
        out_specs=P(None, None, "gx", "gy", "gz"),
        check_vma=False,
    )
```

time: 129 us -> 64.6 us (0.50); the launches traced: 127 us -> 64.3 us
  Pallas kernels: 0 us -> 43 us
  starting transfers between devices: 35.5 us -> 0 us
  local copies, waits for them, and re-layouts: 53 us -> 19.9 us
  matrix products: 21.2 us -> 0 us
  other arithmetic: 9.56 us -> 1.25 us
  waiting for transfers between devices: 7.42 us -> 0 us
    pallas_call x0 -> x1, Pallas kernels: none -> 43 us  [shards(): pl.pallas_call(kernel, out_shape=jax.ShapeDtypeStruct((LX, LY, LP, 2 * HA...]
    ppermute x18 -> x0, starting transfers between devices: 35.5 us -> none  [the longest x9 20.2 us: extended(): lax.ppermute(tail, axis, [(i, (i + 1) % count) for i in range(count)])]
    dot_general x27 -> x0, matrix products: 21.2 us -> none  [conv_valid(): jnp.einsum('oc,bcxyz->boxyz', matrix, stacked, preferred_element_type=jnp...]
    slice x22 -> x0, local copies, waits for them, and re-layouts: 17.8 us -> none  [the longest x9 13.1 us: conv_valid(): padded[:, :, along_x:along_x + width, along_y:along_y + height, along_z:a...]
    transpose x30 -> x1, local copies, waits for them, and re-layouts: 17.4 us -> 3.31 us  [shards(): jnp.transpose(cells, (1, 2, 3, 4, 0)).reshape(LX, LY, LP, 2 * channels)]
    concatenate x9 -> x2, other arithmetic: 9.51 us -> 0.92 us  [toeplitz(): block = jnp.concatenate([lower, upper], axis=3)]
    reshape x0 -> x4, local copies, waits for them, and re-layouts: none -> 8.23 us  [the longest x2 3.67 us: shards(): result = result.reshape(LX, LY, LP, 2, channels)]
    ppermute x18 -> x0, waiting for transfers between devices: 7.42 us -> none  [the longest x9 7.4 us: extended(): lax.ppermute(tail, axis, [(i, (i + 1) % count) for i in range(count)])]
  transfers between devices with their start and end apart: 18 -> 0, of which waited for: 3 -> 0; matrix products, arithmetic and copies ran while one was open for 22% -> 0% of each run, Pallas kernels for 0% -> 0%
where the time goes in v1:
time: 64.6 us; the launch traced here: 64.3 us
  Pallas kernels  43 us (67%)
  local copies, waits for them, and re-layouts  19.9 us (31%)
  other arithmetic  1.25 us (2%)
    pallas_call x1, Pallas kernels, shards(): pl.pallas_call(kernel, out_shape=jax.ShapeDtypeStruct((LX, LY, LP, 2 * HA...  43 us
    unnamed x22, local copies, waits for them, and re-layouts  6.24 us
    reshape x2, local copies, waits for them, and re-layouts, shards(): result = result.reshape(LX, LY, LP, 2, channels)  3.67 us
    transpose x1, local copies, waits for them, and re-layouts, shards(): jnp.transpose(cells, (1, 2, 3, 4, 0)).reshape(LX, LY, LP, 2 * channels)  3.31 us
    reshape x1, local copies, waits for them, and re-layouts, shards(): jnp.transpose(cells, (1, 2, 3, 4, 0)).reshape(LX, LY, LP, 2 * channels)  2.6 us
    reshape x1, local copies, waits for them, and re-layouts, shards(): jnp.transpose(result, (4, 0, 1, 2, 3)).reshape(1, channels, LX, LY, 2 * LP)  1.97 us
    another operation x2, local copies, waits for them, and re-layouts, shards(): jnp.stack([toeplitz(k) for k in (kernel_one, kernel_two, kernel_three)])  1.69 us

profile of v1, /device:TPU:1, one launch (start us, length us, event | category | flops | bytes accessed | tf_op | source)
XLA Modules:
  0.0 64.3 jit_solution(2962950283078822194)
XLA Ops:
  0.0 1.3 %copy.17 = bf16[3,3,3,64,64]{3,4,1,0,2:T(8,128)(2,1)S(1)} copy(bf16[3,3,3,64,64]{4,3,2,1,0:T(8,128)(2,1)} %param.12) | data formatting | bytes 442368 | tf_op args[5]
  1.4 0.2 copy.15
  1.7 0.6 fusion.1
  2.3 0.0 copy-start.5
  2.3 1.6 %pad_bitcast_fusion = (bf16[1,3,5,256,128]{4,3,2,1,0:T(8,128)(2,1)}, bf16[1,3,5,256,128]{4,3,2,1,0:T(8,128)(2,1)}) fusion(bf16[3,3,256,128]{3,2,1,0:T(8,128)(2,1)S(1)} %get-tuple-element.15, bf16[3,3,256,128]{3,2,1,0:T(8,128)(2,1)S(1)} %get-tuple-element.14), kind=kLoop, calls=%fused_computation.7 | loop fusion | bytes 3145728 | tf_op jit(solution)/shard_map/stack | solution.py:191
  3.9 0.2 copy.16
  4.2 0.3 fusion.3
  4.5 0.1 pad_bitcast_fusion.1
  4.6 0.7 %copy-done.1 = bf16[1,3,5,256,128]{4,3,2,1,0:T(8,128)(2,1)S(1)} copy-done((bf16[1,3,5,256,128]{4,3,2,1,0:T(8,128)(2,1)S(1)}, bf16[1,3,5,256,128]{4,3,2,1,0:T(8,128)(2,1)}, u32[]{:S(2)}) %copy-start.1) | copy-done | bytes 983064
  5.4 0.3 copy-done.2
  5.7 0.3 pad_maximum_fusion.weights
  6.0 0.7 %copy-done.3 = bf16[1,64,4,8,128]{4,3,2,1,0:T(8,128)(2,1)S(1)} copy-done((bf16[1,64,4,8,128]{4,3,2,1,0:T(8,128)(2,1)S(1)}, bf16[1,64,4,8,128]{4,3,2,1,0:T(8,128)(2,1)}, u32[]{:S(2)}) %copy-start.3) | copy-done | bytes 524312
  6.7 1.9 %copy.13 = bf16[1,64,4,8,128]{1,3,4,2,0:T(8,128)(2,1)} copy(bf16[1,64,4,8,128]{4,3,2,1,0:T(8,128)(2,1)S(1)} %copy-done.3) | data formatting | bytes 1048576 | tf_op args[0]
  8.6 3.3 %copy.14 = bf16[4,8,64,2,64]{4,3,2,1,0:T(2,128)(2,1)} copy(bf16[4,8,64,2,64]{4,1,3,2,0:T(8,128)(2,1)} %bitcast.36) | data formatting | bytes 1048576 | tf_op jit(solution)/shard_map/transpose | solution.py:190
  11.9 2.6 %reshape.16.field = bf16[4,8,64,128]{3,2,1,0:T(8,128)(2,1)S(1)} reshape(bf16[4,8,64,2,64]{4,3,2,1,0:T(2,128)(2,1)} %copy.14) | data formatting | bytes 1048576 | tf_op jit(solution)/shard_map/reshape | solution.py:190
  14.5 0.1 stack_broadcast_in_dim_tile.10
  14.6 0.1 stack_broadcast_in_dim_tile.11
  14.7 0.1 stack_broadcast_in_dim_tile.9
  14.8 43.0 %shard_map.73 = bf16[4,8,64,128]{3,2,1,0:T(8,128)(2,1)S(1)} custom-call(bf16[4,8,64,128]{3,2,1,0:T(8,128)(2,1)S(1)} %reshape.16.field, bf16[3,3,5,256,128]{4,3,2,1,0:T(8,128)(2,1)S(1)} %pad_maximum_fusion.weights, f32[3,1,256]{2,1,0:T(1,128)S(1)} %pad_maximum_fusion.7.bias), custom_call_target="tpu_custom_call" | custom-call | tf_op jit(solution)/shard_map/pallas_call | solution.py:194
  57.8 0.0 copy-start
  57.9 0.8 %copy-done = bf16[4,8,64,128]{3,2,1,0:T(8,128)(2,1)} copy-done((bf16[4,8,64,128]{3,2,1,0:T(8,128)(2,1)}, bf16[4,8,64,128]{3,2,1,0:T(8,128)(2,1)S(1)}, u32[]{:S(2)}) %copy-start) | copy-done | bytes 524312
  58.6 2.4 %reshape.17 = bf16[4,8,64,2,64]{4,3,2,1,0:T(2,128)(2,1)S(1)} reshape(bf16[4,8,64,128]{3,2,1,0:T(8,128)(2,1)} %copy-done) | data formatting | bytes 1048576 | tf_op jit(solution)/shard_map/reshape | solution.py:214
  61.1 1.2 %copy.18 = bf16[4,8,64,2,64]{4,1,3,2,0:T(8,128)(2,1)S(1)} copy(bf16[4,8,64,2,64]{4,3,2,1,0:T(2,128)(2,1)S(1)} %reshape.17) | data formatting | bytes 1048576 | tf_op jit(solution)/shard_map/reshape | solution.py:214
  62.3 2.0 %copy.19 = bf16[1,64,4,8,128]{4,3,2,1,0:T(8,128)(2,1)} copy(bf16[1,64,4,8,128]{1,3,4,2,0:T(8,128)(2,1)S(1)} %bitcast.35) | data formatting | bytes 1048576 | tf_op jit(solution)/shard_map/reshape | solution.py:215
  (20 shorter events, 0.2 us)
Async XLA Ops:
  0.0 1.4 %copy-start.4 = (bf16[3,3,3,64,64]{4,3,2,1,0:T(8,128)(2,1)S(1)}, bf16[3,3,3,64,64]{4,3,2,1,0:T(8,128)(2,1)}, u32[]{:S(2)}) copy-start(bf16[3,3,3,64,64]{4,3,2,1,0:T(8,128)(2,1)} %param.8) | copy-start | bytes 663556
  2.3 1.6 %copy-start.5 = (bf16[3,3,3,64,64]{4,3,2,1,0:T(8,128)(2,1)S(1)}, bf16[3,3,3,64,64]{4,3,2,1,0:T(8,128)(2,1)}, u32[]{:S(2)}) copy-start(bf16[3,3,3,64,64]{4,3,2,1,0:T(8,128)(2,1)} %param.10) | copy-start | bytes 663556
  4.2 1.2 %copy-start.1 = (bf16[1,3,5,256,128]{4,3,2,1,0:T(8,128)(2,1)S(1)}, bf16[1,3,5,256,128]{4,3,2,1,0:T(8,128)(2,1)}, u32[]{:S(2)}) copy-start(bf16[1,3,5,256,128]{4,3,2,1,0:T(8,128)(2,1)} %get-tuple-element.16) | copy-start | bytes 2949124
  4.2 1.5 %copy-start.2 = (bf16[1,3,5,256,128]{4,3,2,1,0:T(8,128)(2,1)S(1)}, bf16[1,3,5,256,128]{4,3,2,1,0:T(8,128)(2,1)}, u32[]{:S(2)}) copy-start(bf16[1,3,5,256,128]{4,3,2,1,0:T(8,128)(2,1)} %get-tuple-element.17) | copy-start | bytes 2949124
  5.7 1.0 %copy-start.3 = (bf16[1,64,4,8,128]{4,3,2,1,0:T(8,128)(2,1)S(1)}, bf16[1,64,4,8,128]{4,3,2,1,0:T(8,128)(2,1)}, u32[]{:S(2)}) copy-start(bf16[1,64,4,8,128]{4,3,2,1,0:T(8,128)(2,1)} %param.7) | copy-start | bytes 1572868
  11.9 2.6 %copy-start.6 = (f32[64]{0:T(128)S(1)}, f32[64]{0:T(128)}, u32[]{:S(2)}) copy-start(f32[64]{0:T(128)} %param.11) | copy-start | bytes 772
  11.9 2.7 %copy-start.7 = (f32[64]{0:T(128)S(1)}, f32[64]{0:T(128)}, u32[]{:S(2)}) copy-start(f32[64]{0:T(128)} %param.13) | copy-start | bytes 772
  11.9 2.8 %copy-start.8 = (f32[64]{0:T(128)S(1)}, f32[64]{0:T(128)}, u32[]{:S(2)}) copy-start(f32[64]{0:T(128)} %param.9) | copy-start | bytes 772
  57.8 0.8 %copy-start = (bf16[4,8,64,128]{3,2,1,0:T(8,128)(2,1)}, bf16[4,8,64,128]{3,2,1,0:T(8,128)(2,1)S(1)}, u32[]{:S(2)}) copy-start(bf16[4,8,64,128]{3,2,1,0:T(8,128)(2,1)S(1)} %shard_map.73) | copy-start | bytes 1572868

commit v2 on v0

v2 whole, which is shorter than its diff:
```python
import jax
import jax.numpy as jnp
from jax import lax
from jax.experimental import pallas as pl
from jax.experimental.pallas import tpu as pltpu
from jax.sharding import PartitionSpec as P

MESH = pl.DeviceIdType.MESH
AXES = ("gx", "gy", "gz")
C = 64
W = 2 * C
LX, LY, LP = 4, 8, 64
LZ = 2 * LP
PAIRS = LY // 2
INNER, OUTER = "inner", "outer"
BF = jnp.bfloat16
F32 = jnp.float32


def plan():
    entries = []
    for dx in (-1, 1):
        entries.append(((dx, 0, 0), OUTER, None))
        for dy in (-1, 1):
            entries.append(((dx, dy, 0), OUTER, None))
    for dz in (-1, 1):
        for dx in (-1, 1, 0):
            for dy in (-1, 0, 1):
                entries.append(((dx, dy, dz), OUTER, None))
    for dy in (-1, 1):
        entries.append(((0, dy, 0), OUTER, (1, 1)))
        entries.append(((0, dy, 0), OUTER, (LX, 1)))
        entries.append(((0, dy, 0), INNER, (2, LX - 2)))
    return entries


PLAN = plan()
WAYS = sorted({way for way, _, _ in PLAN})


def neighbour(way):
    ids = []
    for axis, step in zip(AXES, way):
        count = lax.axis_size(axis)
        ids.append(lax.rem(lax.axis_index(axis) + step + count, count))
    return tuple(ids)


def message(layer, which, a, zs, zr, send, recv):
    (dx, dy, dz), _, planes = PLAN[which]
    if dz == 0:
        across = pl.ds(*planes) if dx == 0 else None
        near_x = {1: LX, -1: 1, 0: across}[dx]
        far_x = {1: 0, -1: LX + 1, 0: across}[dx]
        near_y = {1: LY, -1: 1, 0: pl.ds(1, LY)}[dy]
        far_y = {1: 0, -1: LY + 1, 0: pl.ds(1, LY)}[dy]
        source = a.at[layer, near_x, near_y]
        target = a.at[layer, far_x, far_y]
    else:
        side, other = (1, 0) if dz == 1 else (0, 1)
        source = zs.at[layer, side]
        target = zr.at[layer, other, 1 - dx, 1 - dy]
        if dx != 0:
            plane = LX - 1 if dx == 1 else 0
            source = source.at[plane]
            target = target.at[plane]
    return pltpu.make_async_remote_copy(
        src_ref=source,
        dst_ref=target,
        send_sem=send.at[layer, which],
        recv_sem=recv.at[layer, which],
        device_id=neighbour((dx, dy, dz)),
        device_id_type=MESH,
    )


def kernel(
    field, k_one, k_two, k_three, b_one, b_two, b_three, out,
    raw, wide, taps, weights, bias, spread, gather, a, b, zs, zr, edge, halo, stage, thin,
    send, recv, field_sem, tap_sem, out_sem, bias_sem,
):
    field_in = [pltpu.make_async_copy(field.at[0, :, x], raw.at[x], field_sem.at[x]) for x in range(LX)]
    taps_in = [pltpu.make_async_copy(k, taps.at[i], tap_sem.at[i]) for i, k in enumerate((k_one, k_two, k_three))]
    for x in (0, LX - 1, *range(1, LX - 1)):
        field_in[x].start()
    bias_in = [pltpu.make_async_copy(v, thin.at[i], bias_sem.at[i]) for i, v in enumerate((b_one, b_two, b_three))]
    for copy in taps_in + bias_in:
        copy.start()
    barrier = pltpu.get_barrier_semaphore()
    for way in WAYS:
        pl.semaphore_signal(barrier, inc=1, device_id=neighbour(way), device_id_type=MESH)

    def one_hot(natural, paired):
        slab, z = natural // LZ, natural % LZ
        parity, other, pair = paired // W, (paired // LP) % 2, paired % LP
        return ((slab == other) & (z == 2 * pair + parity)).astype(F32).astype(BF)

    first = lax.broadcasted_iota(jnp.int32, (2 * LZ, 2 * W), 0)
    second = lax.broadcasted_iota(jnp.int32, (2 * LZ, 2 * W), 1)
    spread[...] = one_hot(first, second)
    gather[...] = one_hot(second, first)

    def relay_in(x):
        field_in[x].wait()
        wide[...] = raw[x].astype(F32).reshape(C * LY, LZ)
        rows = []
        for j in range(PAIRS):
            pair = [wide[pl.ds(2 * j + s, C, stride=LY), :].astype(BF) for s in range(2)]
            rows.append(jnp.concatenate(pair, axis=1))
        split = jnp.dot(jnp.concatenate(rows, axis=0), spread[...], preferred_element_type=F32).astype(BF)
        for j in range(PAIRS):
            block = split[j * C : (j + 1) * C]
            cells = jnp.concatenate([block[:, :W], block[:, W:]], axis=0).T
            for s in range(2):
                y = 2 * j + s
                slab = cells[s * LP : (s + 1) * LP]
                a[0, x + 1, y + 1] = slab
                edge[0, x, y : y + 1, :] = slab[:16].astype(F32)[:1]
                edge[1, x, y : y + 1, :] = slab[LP - 16 :].astype(F32)[15:]

    def pack_edges(layer, planes):
        for side in range(2):
            for x in planes:
                zs[layer, side, x] = edge[side, x].astype(BF)

    def start(layer, choose):
        for which, entry in enumerate(PLAN):
            if choose(entry):
                message(layer, which, a, zs, zr, send, recv).start()

    def arrive(layer, choose):
        for which, entry in enumerate(PLAN):
            if choose(entry):
                message(layer, which, a, zs, zr, send, recv).wait_recv()

    def crosses_x(entry):
        return entry[0][0] != 0

    def stays_outer(entry):
        return entry[0][0] == 0 and entry[1] == OUTER

    def stays_inner(entry):
        return entry[0][0] == 0 and entry[1] == INNER

    outer_planes = (0, LX - 1)
    inner_planes = tuple(range(1, LX - 1))

    for x in outer_planes:
        relay_in(x)
    pack_edges(0, outer_planes)
    pl.semaphore_wait(barrier, len(WAYS))
    start(0, crosses_x)
    for x in inner_planes:
        relay_in(x)
    pack_edges(0, inner_planes)
    start(0, stays_outer)
    start(0, stays_inner)

    none = jnp.zeros((C, C), BF)
    for layer in range(3):
        taps_in[layer].wait()
        bias_in[layer].wait()
        twice = jnp.concatenate([thin[layer], thin[layer]], axis=1)
        bias[layer] = jnp.concatenate([twice, twice], axis=1)

        def band(i, carry):
            along_x, along_y = i // 3, i % 3
            tap = [taps[layer, along_x, along_y, f] for f in range(3)]
            order = ((tap[1], tap[0]), (tap[2], tap[1]), (none, tap[2]), (tap[0], none))
            for k, (low, high) in enumerate(order):
                block = jnp.concatenate([low, high], axis=0).T
                weights[layer, i, k * C : (k + 1) * C, :] = block
            return carry

        lax.fori_loop(0, 9, band, 0)

    lane = lax.broadcasted_iota(jnp.int32, (LP, W), 1)
    row = lax.broadcasted_iota(jnp.int32, (LP, W), 0)
    even = lane < C
    ends = (even & (row == LP - 1)) | (~even & (row == 0))
    even_row = lax.broadcasted_iota(jnp.int32, (LY, W), 1) < C
    blank = jnp.zeros((2 * W, W), BF)

    for layer in range(3):

        def shift(x, ix, sx):
            for iy in range(3):
                rows = jnp.where(even_row, zr[layer, 1, ix, iy, sx].astype(F32), zr[layer, 0, ix, iy, sx].astype(F32))
                if iy == 0:
                    halo[7:8, :] = rows[7:8]
                elif iy == 1:
                    halo[8:16, :] = rows
                else:
                    halo[16:17, :] = rows[0:1]
            for y in range(LY + 2):
                slab = a[layer, x, y].astype(F32)
                up = pltpu.roll(slab, LP - 1, 0)
                down = pltpu.roll(slab, 1, 0)
                fill = jnp.broadcast_to(halo[y + 7 : y + 8, :], (LP, W))
                b[x, y] = jnp.where(ends, fill, jnp.where(even, up, down)).astype(BF)

        def shift_local(i, carry):
            shift(i + 1, 1, i)
            return carry

        def plane(x):
            total = None
            for along_x in range(3):
                for t in range(4):
                    left = jnp.concatenate([a[layer, x + along_x, t + 2 * j] for j in range(PAIRS)], axis=0)
                    right = jnp.concatenate([b[x + along_x, t + 2 * j] for j in range(PAIRS)], axis=0)
                    low = weights[layer, 3 * along_x + t] if t < 3 else blank
                    high = weights[layer, 3 * along_x + t - 1] if t > 0 else blank
                    term = jnp.dot(
                        jnp.concatenate([left, right], axis=1),
                        jnp.concatenate([low, high], axis=1),
                        preferred_element_type=F32,
                    )
                    total = term if total is None else total + term
            total = total + bias[layer]
            value = 0.5 * total * (1.0 + lax.erf(total * 0.7071067811865476))
            if layer < 2:
                for j in range(PAIRS):
                    for s in range(2):
                        y = 2 * j + s
                        slab = value[j * LP : (j + 1) * LP, s * W : (s + 1) * W]
                        a[layer + 1, x + 1, y + 1] = slab.astype(BF)
                        edge[0, x, y : y + 1, :] = slab[0:1]
                        edge[1, x, y : y + 1, :] = slab[LP - 1 :]
            else:
                rounded = value.astype(BF)
                rows = []
                for j in range(PAIRS):
                    block = rounded[j * LP : (j + 1) * LP]
                    turned = jnp.concatenate([block[:, :W], block[:, W:]], axis=0).T
                    rows.append(jnp.concatenate([turned[:C], turned[C:]], axis=1))
                merged = jnp.dot(jnp.concatenate(rows, axis=0), gather[...], preferred_element_type=F32)
                for j in range(PAIRS):
                    for s in range(2):
                        wide[pl.ds(2 * j + s, C, stride=LY), :] = merged[j * C : (j + 1) * C, s * LZ : (s + 1) * LZ]
                stage[x] = wide[...].reshape(C, LY, LZ).astype(BF)
                pltpu.make_async_copy(stage.at[x], out.at[0, :, x], out_sem.at[x]).start()

        arrive(layer, lambda entry: not crosses_x(entry))
        lax.fori_loop(0, LX, shift_local, 0)
        for x in inner_planes:
            plane(x)
        if layer < 2:
            pack_edges(layer + 1, inner_planes)
            start(layer + 1, stays_inner)
        arrive(layer, crosses_x)
        shift(0, 0, LX - 1)
        shift(LX + 1, 2, 0)
        for x in outer_planes:
            plane(x)
        if layer < 2:
            pack_edges(layer + 1, outer_planes)
            start(layer + 1, crosses_x)
            start(layer + 1, stays_outer)

    for layer in range(3):
        for which in range(len(PLAN)):
            message(layer, which, a, zs, zr, send, recv).wait_send()
    for x in range(LX):
        pltpu.make_async_copy(stage.at[x], out.at[0, :, x], out_sem.at[x]).wait()


def shards(field, kernel_one, bias_one, kernel_two, bias_two, kernel_three, bias_three):
    hbm = pl.BlockSpec(memory_space=pltpu.HBM)
    return pl.pallas_call(
        kernel,
        out_shape=jax.ShapeDtypeStruct(field.shape, BF),
        in_specs=[hbm] * 7,
        out_specs=hbm,
        scratch_shapes=[
            pltpu.VMEM((LX, C, LY, LZ), BF),
            pltpu.VMEM((C * LY, LZ), F32),
            pltpu.VMEM((3, 3, 3, 3, C, C), BF),
            pltpu.VMEM((3, 9, 2 * W, W), BF),
            pltpu.VMEM((3, 1, 2 * W), F32),
            pltpu.VMEM((2 * LZ, 2 * W), BF),
            pltpu.VMEM((2 * W, 2 * LZ), BF),
            pltpu.VMEM((3, LX + 2, LY + 2, LP, W), BF),
            pltpu.VMEM((LX + 2, LY + 2, LP, W), BF),
            pltpu.VMEM((3, 2, LX, LY, W), BF),
            pltpu.VMEM((3, 2, 3, 3, LX, LY, W), BF),
            pltpu.VMEM((2, LX, LY, W), F32),
            pltpu.VMEM((24, W), F32),
            pltpu.VMEM((LX, C, LY, LZ), BF),
            pltpu.VMEM((3, 1, C), F32),
            pltpu.SemaphoreType.DMA((3, len(PLAN))),
            pltpu.SemaphoreType.DMA((3, len(PLAN))),
            pltpu.SemaphoreType.DMA((LX,)),
            pltpu.SemaphoreType.DMA((3,)),
            pltpu.SemaphoreType.DMA((LX,)),
            pltpu.SemaphoreType.DMA((3,)),
        ],
        compiler_params=pltpu.CompilerParams(
            collective_id=0, has_side_effects=True, vmem_limit_bytes=65_900_000
        ),
    )(
        field,
        kernel_one,
        kernel_two,
        kernel_three,
        bias_one.reshape(1, C),
        bias_two.reshape(1, C),
        bias_three.reshape(1, C),
    )


def solution(mesh):
    return jax.shard_map(
        shards,
        mesh=mesh,
        in_specs=(P(None, None, "gx", "gy", "gz"), P(), P(), P(), P(), P(), P()),
        out_specs=P(None, None, "gx", "gy", "gz"),
        check_vma=False,
    )
```

time: 129 us -> 41.6 us (0.32); the launches traced: 127 us -> 41.4 us
  local copies, waits for them, and re-layouts: 53 us -> 1.87 us
  Pallas kernels: 0 us -> 39.5 us
  starting transfers between devices: 35.5 us -> 0 us
  matrix products: 21.2 us -> 0 us
  other arithmetic: 9.56 us -> 0 us
  waiting for transfers between devices: 7.42 us -> 0 us
    pallas_call x0 -> x1, Pallas kernels: none -> 39.5 us  [shards(): pl.pallas_call(kernel, out_shape=jax.ShapeDtypeStruct(field.shape, BF), i...]
    ppermute x18 -> x0, starting transfers between devices: 35.5 us -> none  [the longest x9 20.2 us: extended(): lax.ppermute(tail, axis, [(i, (i + 1) % count) for i in range(count)])]
    dot_general x27 -> x0, matrix products: 21.2 us -> none  [conv_valid(): jnp.einsum('oc,bcxyz->boxyz', matrix, stacked, preferred_element_type=jnp...]
    slice x22 -> x0, local copies, waits for them, and re-layouts: 17.8 us -> none  [the longest x9 13.1 us: conv_valid(): padded[:, :, along_x:along_x + width, along_y:along_y + height, along_z:a...]
    transpose x30 -> x0, local copies, waits for them, and re-layouts: 17.4 us -> none  [conv_valid(): jnp.transpose(kernel[along_x, along_y], (1, 0, 2))]
    unnamed x101 -> x1, local copies, waits for them, and re-layouts: 11.4 us -> 1.87 us
    concatenate x9 -> x0, other arithmetic: 9.51 us -> none  [extended(): jnp.concatenate([lax.ppermute(tail, axis, [(i, (i + 1) % count) for i in...]
    ppermute x18 -> x0, waiting for transfers between devices: 7.42 us -> none  [the longest x9 7.4 us: extended(): lax.ppermute(tail, axis, [(i, (i + 1) % count) for i in range(count)])]
  transfers between devices with their start and end apart: 18 -> 0, of which waited for: 3 -> 0; matrix products, arithmetic and copies ran while one was open for 22% -> 0% of each run, Pallas kernels for 0% -> 0%
where the time goes in v2:
time: 41.6 us; the launch traced here: 41.4 us
  Pallas kernels  39.5 us (95%)
  local copies, waits for them, and re-layouts  1.87 us (4%)
    pallas_call x1, Pallas kernels, shards(): pl.pallas_call(kernel, out_shape=jax.ShapeDtypeStruct(field.shape, BF), i...  39.5 us
    unnamed x1, local copies, waits for them, and re-layouts  1.87 us

profile of v2, /device:TPU:1, one launch (start us, length us, event | category | flops | bytes accessed | tf_op | source)
XLA Modules:
  0.0 41.4 jit_solution(3375674407988924329)
XLA Ops:
  0.0 39.5 %shard_map.73 = bf16[1,64,4,8,128]{4,3,2,1,0:T(8,128)(2,1)} custom-call(bf16[1,64,4,8,128]{4,3,2,1,0:T(8,128)(2,1)} %field.1, bf16[3,3,3,64,64]{4,3,2,1,0:T(8,128)(2,1)} %k_one.1, bf16[3,3,3,64,64]{4,3,2,1,0:T(8,128)(2,1)} %k_two.1, bf16[3,3,3,64,64]{4,3,2,1,0:T(8,128)(2,1)} %k_three.1, f32[1,64]{1,0:T(1,128)} %bitcast.3, f32[1,64]{1,0:T(1,128)} %bitcast.4, ...), custom_call_target="tpu_custom_call" | custom-call | tf_op jit(solution)/shard_map/pallas_call | solution.py:270
  39.5 1.9 %copy.9 = bf16[1,64,4,8,128]{4,3,2,1,0:T(8,128)(2,1)} copy(bf16[1,64,4,8,128]{4,3,2,1,0:T(8,128)(2,1)} %shard_map.73) | data formatting | bytes 1048576

commit v3 on v2

v3 whole, which is shorter than its diff:
```python
import jax
import jax.numpy as jnp
from jax import lax
from jax.experimental import pallas as pl
from jax.experimental.pallas import tpu as pltpu
from jax.sharding import PartitionSpec as P

MESH = pl.DeviceIdType.MESH
AXES = ("gx", "gy", "gz")
C = 64
W = 2 * C
LX, LY, LP = 4, 8, 64
LZ = 2 * LP
PAIRS = LY // 2
BF = jnp.bfloat16
F32 = jnp.float32
HIGH = {1: 1, -1: 0}


def plan():
    both = (-1, 1)
    entries = [((dx, dy, dz), 1, None) for dx in both for dy in both for dz in both]
    entries += [((dx, dy, 0), 1, None) for dx in both for dy in both]
    entries += [((0, dy, 0), 1, piece) for dy in both for piece in ((1, 1), (LX, 1))]
    entries += [((dx, 0, 0), 1, (1, 2)) for dx in both]
    entries += [((dx, 0, dz), 2, None) for dx in both for dz in both]
    entries += [((0, dy, dz), 2, None) for dy in both for dz in both]
    entries += [((0, 0, dz), 2, None) for dz in both]
    entries += [((dx, 0, 0), 2, (LY - 1, 2)) for dx in both]
    entries += [((0, dy, 0), 3, (2, LX - 2)) for dy in both]
    entries += [((dx, 0, 0), 4, (3, LY - 4)) for dx in both]
    return entries


PLAN = plan()
WAYS = sorted({way for way, _, _ in PLAN})


def neighbour(way):
    ids = []
    for axis, step in zip(AXES, way):
        count = lax.axis_size(axis)
        ids.append(lax.rem(lax.axis_index(axis) + step + count, count))
    return tuple(ids)


def message(layer, which, a, out_rows, in_rows, send, recv):
    (dx, dy, dz), _, piece = PLAN[which]
    if dz == 0:
        near_x = {1: LX, -1: 1}.get(dx)
        far_x = {1: 0, -1: LX + 1}.get(dx)
        near_y = {1: LY, -1: 1}.get(dy)
        far_y = {1: 0, -1: LY + 1}.get(dy)
        if dx == 0:
            near_x = far_x = pl.ds(*piece)
        if dy == 0:
            near_y = far_y = pl.ds(*piece)
        source = a.at[layer, near_x, near_y]
        target = a.at[layer, far_x, far_y]
    else:
        kind = (dx != 0) + 2 * (dy != 0)
        source = out_rows[kind].at[layer, HIGH[dz]]
        target = in_rows[kind].at[layer, HIGH[-dz]]
        for step in (dx, dy):
            if step != 0:
                source = source.at[HIGH[step]]
                target = target.at[HIGH[-step]]
    return pltpu.make_async_remote_copy(
        src_ref=source,
        dst_ref=target,
        send_sem=send.at[layer, which],
        recv_sem=recv.at[layer, which],
        device_id=neighbour((dx, dy, dz)),
        device_id_type=MESH,
    )


def kernel(
    field, k_one, k_two, k_three, b_one, b_two, b_three, out,
    raw, wide, taps, weights, bias, spread, gather, a, b,
    z_all, z_x, z_y, z_xy, r_all, r_x, r_y, r_xy, e_all, e_y, e_xy, halo, thin,
    send, recv, field_sem, tap_sem, bias_sem,
):
    out_rows = (z_all, z_x, z_y, z_xy)
    in_rows = (r_all, r_x, r_y, r_xy)
    field_in = [pltpu.make_async_copy(field.at[0, :, x], raw.at[x], field_sem.at[x]) for x in range(LX)]
    taps_in = [pltpu.make_async_copy(k, taps.at[i], tap_sem.at[i]) for i, k in enumerate((k_one, k_two, k_three))]
    for x in (0, LX - 1, *range(1, LX - 1)):
        field_in[x].start()
    bias_in = [pltpu.make_async_copy(v, thin.at[i], bias_sem.at[i]) for i, v in enumerate((b_one, b_two, b_three))]
    for copy in taps_in + bias_in:
        copy.start()
    barrier = pltpu.get_barrier_semaphore()
    for way in WAYS:
        pl.semaphore_signal(barrier, inc=1, device_id=neighbour(way), device_id_type=MESH)

    def one_hot(natural, paired):
        slab, z = natural // LZ, natural % LZ
        parity, other, pair = paired // W, (paired // LP) % 2, paired % LP
        return ((slab == other) & (z == 2 * pair + parity)).astype(F32).astype(BF)

    first = lax.broadcasted_iota(jnp.int32, (2 * LZ, 2 * W), 0)
    second = lax.broadcasted_iota(jnp.int32, (2 * LZ, 2 * W), 1)
    spread[...] = one_hot(first, second)
    gather[...] = one_hot(second, first)

    e_y[...] = jnp.zeros_like(e_y)
    e_xy[...] = jnp.zeros_like(e_xy)

    def keep_rows(x, y, rows):
        for side in range(2):
            e_all[side, x, y : y + 1, :] = rows[side]
            if y in (0, LY - 1):
                e_y[side, y // (LY - 1), x : x + 1, :] = rows[side]
                if x in (0, LX - 1):
                    e_xy[side, x // (LX - 1), y // (LY - 1), 0:1, :] = rows[side]

    def relay_in(x):
        field_in[x].wait()
        wide[x] = raw[x].astype(F32).reshape(C * LY, LZ)
        rows = []
        for j in range(PAIRS):
            pair = [wide[x, pl.ds(2 * j + s, C, stride=LY), :].astype(BF) for s in range(2)]
            rows.append(jnp.concatenate(pair, axis=1))
        split = jnp.dot(jnp.concatenate(rows, axis=0), spread[...], preferred_element_type=F32).astype(BF)
        for j in range(PAIRS):
            block = split[j * C : (j + 1) * C]
            cells = jnp.concatenate([block[:, :W], block[:, W:]], axis=0).T
            for s in range(2):
                y = 2 * j + s
                slab = cells[s * LP : (s + 1) * LP]
                a[0, x + 1, y + 1] = slab
                keep_rows(x, y, (slab[:16].astype(F32)[:1], slab[LP - 16 :].astype(F32)[15:]))

    def pack(layer, stage):
        for side in range(2):
            for i in range(2):
                if stage == 1:
                    for j in range(2):
                        z_xy[layer, side, i, j] = e_xy[side, i, j].astype(BF)
                elif stage == 2:
                    z_y[layer, side, i] = e_y[side, i].astype(BF)
                    z_x[layer, side, i] = e_all[side, i * (LX - 1)].astype(BF)
            if stage == 2:
                for x in range(LX):
                    z_all[layer, side, x] = e_all[side, x].astype(BF)

    def launch(layer, *stages):
        for stage in stages:
            pack(layer, stage)
        for which, entry in enumerate(PLAN):
            if entry[1] in stages:
                message(layer, which, a, out_rows, in_rows, send, recv).start()

    def arrive(layer, choose):
        for which, entry in enumerate(PLAN):
            if choose(entry):
                message(layer, which, a, out_rows, in_rows, send, recv).wait_recv()

    outer_planes, inner_planes = (0, LX - 1), tuple(range(1, LX - 1))
    outer_pairs, inner_pairs = (0, PAIRS - 1), tuple(range(1, PAIRS - 1))
    whole, middle = ((0, LP),), ((8, LP - 16),)

    def corner_of(planes, pairs):
        return [(x, j) for x in planes for j in pairs]

    for x in outer_planes:
        relay_in(x)
    pl.semaphore_wait(barrier, len(WAYS))
    launch(0, 1)
    for x in inner_planes:
        relay_in(x)
    launch(0, 2, 3, 4)

    none = jnp.zeros((C, C), BF)
    for layer in range(3):
        taps_in[layer].wait()
        bias_in[layer].wait()
        twice = jnp.concatenate([thin[layer], thin[layer]], axis=1)
        bias[layer] = jnp.concatenate([twice, twice], axis=1)

        def band(i, carry):
            along_x, along_y = i // 3, i % 3
            tap = [taps[layer, along_x, along_y, f] for f in range(3)]
            order = ((tap[1], tap[0]), (tap[2], tap[1]), (none, tap[2]), (tap[0], none))
            for k, (low, high) in enumerate(order):
                block = jnp.concatenate([low, high], axis=0).T
                weights[layer, i, k * C : (k + 1) * C, :] = block
            return carry

        lax.fori_loop(0, 9, band, 0)

    lane = lax.broadcasted_iota(jnp.int32, (LP, W), 1)
    row = lax.broadcasted_iota(jnp.int32, (LP, W), 0)
    even = lane < C
    top_row = (~even & (row == 0))[:8]
    low_row = (even & (row == LP - 1))[LP - 8 :]
    even_row = lax.broadcasted_iota(jnp.int32, (LY, W), 1) < C
    blank = jnp.zeros((2 * W, W), BF)

    def merge(ref, layer, *index):
        after, before = ref[(layer, 1, *index)], ref[(layer, 0, *index)]
        return jnp.where(even_row, after.astype(F32), before.astype(F32))

    def shift(layer, x, y):
        slab = a[layer, x, y].astype(F32)
        up = pltpu.roll(slab, LP - 1, 0)
        down = pltpu.roll(slab, 1, 0)
        b[x, y] = jnp.where(even, up, down).astype(BF)

    def patch(x, y):
        fill = jnp.broadcast_to(halo[x, y + 7 : y + 8, :], (8, W))
        top = b[x, y, 0:8, :].astype(F32)
        b[x, y, 0:8, :] = jnp.where(top_row, fill, top).astype(BF)
        low = b[x, y, LP - 8 : LP, :].astype(F32)
        b[x, y, LP - 8 : LP, :] = jnp.where(low_row, fill, low).astype(BF)

    def shift_own(layer):
        def step(i, carry):
            for y in range(LY):
                shift(layer, i + 1, y + 1)
            return carry

        lax.fori_loop(0, LX, step, 0)

    def finish_own(layer):
        for x in range(LX):
            halo[x + 1, 8:16, :] = merge(r_all, layer, x)
            for y in range(1, LY + 1):
                patch(x + 1, y)

    def finish_y(layer):
        for iy, y in enumerate((0, LY + 1)):
            rows = merge(r_y, layer, iy)
            for x in range(LX):
                halo[x + 1, y + 7 : y + 8, :] = rows[x : x + 1]
                shift(layer, x + 1, y)
                patch(x + 1, y)

    def finish_side(layer, ix):
        x = ix * (LX + 1)
        halo[x, 8:16, :] = merge(r_x, layer, ix)
        halo[x, 7:8, :] = merge(r_xy, layer, ix, 0)[0:1]
        halo[x, 16:17, :] = merge(r_xy, layer, ix, 1)[0:1]
        for y in range(LY + 2):
            shift(layer, x, y)
            patch(x, y)

    for layer in range(3):

        def block(places, spans):
            def rows_of(ref, *index):
                return [ref[(*index, pl.ds(low, size), slice(None))] for low, size in spans]

            depth = sum(size for _, size in spans)
            total = None
            for along_x in range(3):
                for t in range(4):
                    left, right = [], []
                    for x, j in places:
                        left += rows_of(a, layer, x + along_x, t + 2 * j)
                        right += rows_of(b, x + along_x, t + 2 * j)
                    low = weights[layer, 3 * along_x + t] if t < 3 else blank
                    high = weights[layer, 3 * along_x + t - 1] if t > 0 else blank
                    term = jnp.dot(
                        jnp.concatenate([jnp.concatenate(left, axis=0), jnp.concatenate(right, axis=0)], axis=1),
                        jnp.concatenate([low, high], axis=1),
                        preferred_element_type=F32,
                    )
                    total = term if total is None else total + term
            total = total + bias[layer]
            value = 0.5 * total * (1.0 + lax.erf(total * 0.7071067811865476))
            if layer < 2:
                for k, (x, j) in enumerate(places):
                    for s in range(2):
                        y = 2 * j + s
                        slab = value[k * depth : (k + 1) * depth, s * W : (s + 1) * W]
                        offset = 0
                        for low, size in spans:
                            a[layer + 1, x + 1, y + 1, low : low + size, :] = slab[offset : offset + size].astype(BF)
                            offset += size
                        if spans[0][0] == 0:
                            keep_rows(x, y, (slab[0:1], slab[depth - 1 :]))
            else:
                rounded = value.astype(BF)
                rows = []
                for k in range(len(places)):
                    part = rounded[k * LP : (k + 1) * LP]
                    turned = jnp.concatenate([part[:, :W], part[:, W:]], axis=0).T
                    rows.append(jnp.concatenate([turned[:C], turned[C:]], axis=1))
                merged = jnp.dot(jnp.concatenate(rows, axis=0), gather[...], preferred_element_type=F32)
                for k, (x, j) in enumerate(places):
                    for s in range(2):
                        wide[x, pl.ds(2 * j + s, C, stride=LY), :] = merged[k * C : (k + 1) * C, s * LZ : (s + 1) * LZ]

        shift_own(layer)
        arrive(layer, lambda entry: entry[0][:2] == (0, 0))
        finish_own(layer)
        if layer == 2:
            block(corner_of(inner_planes, inner_pairs), whole)
        arrive(layer, lambda entry: entry[0][0] == 0 and entry[0][1] != 0)
        finish_y(layer)
        if layer == 2:
            block(corner_of(inner_planes, outer_pairs), whole)
            for x in inner_planes:
                out[0, :, x] = wide[x].reshape(C, LY, LZ).astype(BF)
        arrive(layer, lambda entry: entry[0][0] != 0)
        for ix in range(2):
            finish_side(layer, ix)
        if layer < 2:
            block(corner_of(outer_planes, outer_pairs), whole)
            launch(layer + 1, 1)
            rest = corner_of(outer_planes, inner_pairs) + corner_of(inner_planes, range(PAIRS))
            block(rest, ((0, 8), (LP - 8, 8)))
            launch(layer + 1, 2)
            block(corner_of(inner_planes, outer_pairs), middle)
            launch(layer + 1, 3)
            block(corner_of(outer_planes, inner_pairs), middle)
            launch(layer + 1, 4)
            block(corner_of(inner_planes, inner_pairs), middle)
        else:
            block(corner_of(outer_planes, outer_pairs), whole)
            block(corner_of(outer_planes, inner_pairs), whole)
            for x in outer_planes:
                out[0, :, x] = wide[x].reshape(C, LY, LZ).astype(BF)

    for layer in range(3):
        for which in range(len(PLAN)):
            message(layer, which, a, out_rows, in_rows, send, recv).wait_send()


def shards(field, kernel_one, bias_one, kernel_two, bias_two, kernel_three, bias_three):
    hbm = pl.BlockSpec(memory_space=pltpu.HBM)
    operands = (
        field,
        kernel_one,
        kernel_two,
        kernel_three,
        bias_one.reshape(1, C),
        bias_two.reshape(1, C),
        bias_three.reshape(1, C),
    )
    return pl.pallas_call(
        kernel,
        out_shape=jax.ShapeDtypeStruct(field.shape, BF),
        in_specs=[hbm] * 7,
        out_specs=pl.BlockSpec(memory_space=pltpu.VMEM),
        scratch_shapes=[
            pltpu.VMEM((LX, C, LY, LZ), BF),
            pltpu.VMEM((LX, C * LY, LZ), F32),
            pltpu.VMEM((3, 3, 3, 3, C, C), BF),
            pltpu.VMEM((3, 9, 2 * W, W), BF),
            pltpu.VMEM((3, 1, 2 * W), F32),
            pltpu.VMEM((2 * LZ, 2 * W), BF),
            pltpu.VMEM((2 * W, 2 * LZ), BF),
            pltpu.VMEM((3, LX + 2, LY + 2, LP, W), BF),
            pltpu.VMEM((LX + 2, LY + 2, LP, W), BF),
            pltpu.VMEM((3, 2, LX, LY, W), BF),
            pltpu.VMEM((3, 2, 2, LY, W), BF),
            pltpu.VMEM((3, 2, 2, LY, W), BF),
            pltpu.VMEM((3, 2, 2, 2, LY, W), BF),
            pltpu.VMEM((3, 2, LX, LY, W), BF),
            pltpu.VMEM((3, 2, 2, LY, W), BF),
            pltpu.VMEM((3, 2, 2, LY, W), BF),
            pltpu.VMEM((3, 2, 2, 2, LY, W), BF),
            pltpu.VMEM((2, LX, LY, W), F32),
            pltpu.VMEM((2, 2, LY, W), F32),
            pltpu.VMEM((2, 2, 2, LY, W), F32),
            pltpu.VMEM((LX + 2, 24, W), F32),
            pltpu.VMEM((3, 1, C), F32),
            pltpu.SemaphoreType.DMA((3, len(PLAN))),
            pltpu.SemaphoreType.DMA((3, len(PLAN))),
            pltpu.SemaphoreType.DMA((LX,)),
            pltpu.SemaphoreType.DMA((3,)),
            pltpu.SemaphoreType.DMA((3,)),
        ],
        compiler_params=pltpu.CompilerParams(
            collective_id=0, has_side_effects=True, vmem_limit_bytes=48_000_000
        ),
    )(*[pltpu.with_memory_space_constraint(v, pltpu.HBM) for v in operands])


def solution(mesh):
    return jax.shard_map(
        shards,
        mesh=mesh,
        in_specs=(P(None, None, "gx", "gy", "gz"), P(), P(), P(), P(), P(), P()),
        out_specs=P(None, None, "gx", "gy", "gz"),
        check_vma=False,
    )
```

time: 41.6 us -> 35.4 us (0.85)
  Pallas kernels: 39.5 us -> 34.5 us
  local copies, waits for them, and re-layouts: 1.87 us -> 0.8 us
    pallas_call x1, Pallas kernels: 39.5 us -> 34.5 us  [shards(): pl.pallas_call(kernel, out_shape=jax.ShapeDtypeStruct(field.shape, BF), i...]
    unnamed x1, local copies, waits for them, and re-layouts: 1.87 us -> 0.8 us
where the time goes in v3:
time: 35.4 us; the launch traced here: 35.3 us
  Pallas kernels  34.5 us (97%)
  local copies, waits for them, and re-layouts  0.8 us (2%)
    pallas_call x1, Pallas kernels, shards(): pl.pallas_call(kernel, out_shape=jax.ShapeDtypeStruct(field.shape, BF), i...  34.5 us
    unnamed x1, local copies, waits for them, and re-layouts  0.8 us

profile of v3, /device:TPU:1, one launch (start us, length us, event | category | flops | bytes accessed | tf_op | source)
XLA Modules:
  0.0 35.3 jit_solution(13910872833889500963)
XLA Ops:
  0.0 34.5 %shard_map.73 = bf16[1,64,4,8,128]{4,3,2,1,0:T(8,128)(2,1)S(1)} custom-call(bf16[1,64,4,8,128]{4,3,2,1,0:T(8,128)(2,1)} %field.1, bf16[3,3,3,64,64]{4,3,2,1,0:T(8,128)(2,1)} %k_one.1, bf16[3,3,3,64,64]{4,3,2,1,0:T(8,128)(2,1)} %k_two.1, bf16[3,3,3,64,64]{4,3,2,1,0:T(8,128)(2,1)} %k_three.1, f32[1,64]{1,0:T(1,128)} %bitcast.3, f32[1,64]{1,0:T(1,128)} %bitcast.4, ...), custom_call_target="tpu_custom_call" | custom-call | tf_op jit(solution)/shard_map/pallas_call | solution.py:343
  34.5 0.8 %copy.9 = bf16[1,64,4,8,128]{4,3,2,1,0:T(8,128)(2,1)} copy(bf16[1,64,4,8,128]{4,3,2,1,0:T(8,128)(2,1)S(1)} %shard_map.73) | data formatting | bytes 1048576

commit v4 on v3

--- a/solution.py
+++ b/solution.py
@@ -17,18 +17,22 @@
 HIGH = {1: 1, -1: 0}
 
 
+LAST = (4, LY - 6)
+
+
 def plan():
     both = (-1, 1)
-    entries = [((dx, dy, dz), 1, None) for dx in both for dy in both for dz in both]
+    entries = [((0, dy, 0), 0, (2, LX - 2)) for dy in both]
+    entries += [((dx, dy, dz), 1, None) for dx in both for dy in both for dz in both]
+    entries += [((0, dy, dz), 1, None) for dy in both for dz in both]
     entries += [((dx, dy, 0), 1, None) for dx in both for dy in both]
     entries += [((0, dy, 0), 1, piece) for dy in both for piece in ((1, 1), (LX, 1))]
     entries += [((dx, 0, 0), 1, (1, 2)) for dx in both]
     entries += [((dx, 0, dz), 2, None) for dx in both for dz in both]
-    entries += [((0, dy, dz), 2, None) for dy in both for dz in both]
     entries += [((0, 0, dz), 2, None) for dz in both]
     entries += [((dx, 0, 0), 2, (LY - 1, 2)) for dx in both]
-    entries += [((0, dy, 0), 3, (2, LX - 2)) for dy in both]
-    entries += [((dx, 0, 0), 4, (3, LY - 4)) for dx in both]
+    entries += [((dx, 0, 0), 3, piece) for dx in both for piece in ((3, 1), (LY - 2, 1))]
+    entries += [((dx, 0, 0), 3, LAST) for dx in both]
     return entries
 
 
@@ -83,6 +87,9 @@
 ):
     out_rows = (z_all, z_x, z_y, z_xy)
     in_rows = (r_all, r_x, r_y, r_xy)
+    barrier = pltpu.get_barrier_semaphore()
+    for way in sorted(WAYS, key=lambda w: -sum(map(abs, w))):
+        pl.semaphore_signal(barrier, inc=1, device_id=neighbour(way), device_id_type=MESH)
     field_in = [pltpu.make_async_copy(field.at[0, :, x], raw.at[x], field_sem.at[x]) for x in range(LX)]
     taps_in = [pltpu.make_async_copy(k, taps.at[i], tap_sem.at[i]) for i, k in enumerate((k_one, k_two, k_three))]
     for x in (0, LX - 1, *range(1, LX - 1)):
@@ -90,9 +97,6 @@
     bias_in = [pltpu.make_async_copy(v, thin.at[i], bias_sem.at[i]) for i, v in enumerate((b_one, b_two, b_three))]
     for copy in taps_in + bias_in:
         copy.start()
-    barrier = pltpu.get_barrier_semaphore()
-    for way in WAYS:
-        pl.semaphore_signal(barrier, inc=1, device_id=neighbour(way), device_id_type=MESH)
 
     def one_hot(natural, paired):
         slab, z = natural // LZ, natural % LZ
@@ -138,8 +142,8 @@
                 if stage == 1:
                     for j in range(2):
                         z_xy[layer, side, i, j] = e_xy[side, i, j].astype(BF)
+                    z_y[layer, side, i] = e_y[side, i].astype(BF)
                 elif stage == 2:
-                    z_y[layer, side, i] = e_y[side, i].astype(BF)
                     z_x[layer, side, i] = e_all[side, i * (LX - 1)].astype(BF)
             if stage == 2:
                 for x in range(LX):
@@ -166,11 +170,11 @@
 
     for x in outer_planes:
         relay_in(x)
-    pl.semaphore_wait(barrier, len(WAYS))
-    launch(0, 1)
     for x in inner_planes:
         relay_in(x)
-    launch(0, 2, 3, 4)
+    pl.semaphore_wait(barrier, len(WAYS))
+    for stage in (1, 0, 2, 3):
+        launch(0, stage)
 
     none = jnp.zeros((C, C), BF)
     for layer in range(3):
@@ -223,6 +227,8 @@
 
         lax.fori_loop(0, LX, step, 0)
 
+    late_rows = tuple(range(LAST[0], LAST[0] + LAST[1]))
+
     def finish_own(layer):
         for x in range(LX):
             halo[x + 1, 8:16, :] = merge(r_all, layer, x)
@@ -243,16 +249,22 @@
         halo[x, 7:8, :] = merge(r_xy, layer, ix, 0)[0:1]
         halo[x, 16:17, :] = merge(r_xy, layer, ix, 1)[0:1]
         for y in range(LY + 2):
-            shift(layer, x, y)
-            patch(x, y)
+            if y not in late_rows:
+                shift(layer, x, y)
+                patch(x, y)
+
+    def finish_late(layer):
+        for x in (0, LX + 1):
+            for y in late_rows:
+                shift(layer, x, y)
+                patch(x, y)
 
     for layer in range(3):
 
-        def block(places, spans):
+        def sums(places, spans):
             def rows_of(ref, *index):
                 return [ref[(*index, pl.ds(low, size), slice(None))] for low, size in spans]
 
-            depth = sum(size for _, size in spans)
             total = None
             for along_x in range(3):
                 for t in range(4):
@@ -268,6 +280,10 @@
                         preferred_element_type=F32,
                     )
                     total = term if total is None else total + term
+            return total
+
+        def emit(total, places, spans):
+            depth = sum(size for _, size in spans)
             total = total + bias[layer]
             value = 0.5 * total * (1.0 + lax.erf(total * 0.7071067811865476))
             if layer < 2:
@@ -293,34 +309,39 @@
                     for s in range(2):
                         wide[x, pl.ds(2 * j + s, C, stride=LY), :] = merged[k * C : (k + 1) * C, s * LZ : (s + 1) * LZ]
 
+        def block(*work):
+            values = [sums(*item) for item in work]
+            for value, item in zip(values, work):
+                emit(value, *item)
+
+        outer = corner_of(outer_planes, outer_pairs)
+        ends = ((0, 8), (LP - 8, 8))
         shift_own(layer)
-        arrive(layer, lambda entry: entry[0][:2] == (0, 0))
+        arrive(layer, lambda entry: entry[0][0] == 0)
         finish_own(layer)
-        if layer == 2:
-            block(corner_of(inner_planes, inner_pairs), whole)
-        arrive(layer, lambda entry: entry[0][0] == 0 and entry[0][1] != 0)
         finish_y(layer)
-        if layer == 2:
-            block(corner_of(inner_planes, outer_pairs), whole)
+        if layer < 2:
+            block((corner_of(inner_planes, outer_pairs), whole))
+            launch(layer + 1, 0)
+        else:
+            block((corner_of(inner_planes, inner_pairs), whole), (corner_of(inner_planes, outer_pairs), whole))
             for x in inner_planes:
                 out[0, :, x] = wide[x].reshape(C, LY, LZ).astype(BF)
-        arrive(layer, lambda entry: entry[0][0] != 0)
+        arrive(layer, lambda entry: entry[0][0] != 0 and entry[2] != LAST)
         for ix in range(2):
             finish_side(layer, ix)
         if layer < 2:
-            block(corner_of(outer_planes, outer_pairs), whole)
+            block((outer, whole))
             launch(layer + 1, 1)
-            rest = corner_of(outer_planes, inner_pairs) + corner_of(inner_planes, range(PAIRS))
-            block(rest, ((0, 8), (LP - 8, 8)))
-            launch(layer + 1, 2)
-            block(corner_of(inner_planes, outer_pairs), middle)
-            launch(layer + 1, 3)
-            block(corner_of(outer_planes, inner_pairs), middle)
-            launch(layer + 1, 4)
-            block(corner_of(inner_planes, inner_pairs), middle)
+            arrive(layer, lambda entry: entry[2] == LAST)
+            finish_late(layer)
+            block((corner_of(range(LX), inner_pairs), ends), (corner_of(outer_planes, inner_pairs), middle))
+            launch(layer + 1, 2, 3)
+            block((corner_of(inner_planes, inner_pairs), middle))
         else:
-            block(corner_of(outer_planes, outer_pairs), whole)
-            block(corner_of(outer_planes, inner_pairs), whole)
+            arrive(layer, lambda entry: entry[2] == LAST)
+            finish_late(layer)
+            block((outer, whole), (corner_of(outer_planes, inner_pairs), whole))
             for x in outer_planes:
                 out[0, :, x] = wide[x].reshape(C, LY, LZ).astype(BF)
 

time: 35.4 us -> 33.8 us (0.955)
  Pallas kernels: 34.5 us -> 32.9 us
    pallas_call x1, Pallas kernels: 34.5 us -> 32.9 us  [shards(): pl.pallas_call(kernel, out_shape=jax.ShapeDtypeStruct(field.shape, BF), i...]
where the time goes in v4:
time: 33.8 us; the launch traced here: 33.7 us
  Pallas kernels  32.9 us (97%)
  local copies, waits for them, and re-layouts  0.8 us (2%)
    pallas_call x1, Pallas kernels, shards(): pl.pallas_call(kernel, out_shape=jax.ShapeDtypeStruct(field.shape, BF), i...  32.9 us
    unnamed x1, local copies, waits for them, and re-layouts  0.8 us

profile of v4, /device:TPU:1, one launch (start us, length us, event | category | flops | bytes accessed | tf_op | source)
XLA Modules:
  0.0 33.7 jit_solution(14460369444000657715)
XLA Ops:
  0.0 32.9 %shard_map.73 = bf16[1,64,4,8,128]{4,3,2,1,0:T(8,128)(2,1)S(1)} custom-call(bf16[1,64,4,8,128]{4,3,2,1,0:T(8,128)(2,1)} %field.1, bf16[3,3,3,64,64]{4,3,2,1,0:T(8,128)(2,1)} %k_one.1, bf16[3,3,3,64,64]{4,3,2,1,0:T(8,128)(2,1)} %k_two.1, bf16[3,3,3,64,64]{4,3,2,1,0:T(8,128)(2,1)} %k_three.1, f32[1,64]{1,0:T(1,128)} %bitcast.3, f32[1,64]{1,0:T(1,128)} %bitcast.4, ...), custom_call_target="tpu_custom_call" | custom-call | tf_op jit(solution)/shard_map/pallas_call | solution.py:364
  32.9 0.8 %copy.9 = bf16[1,64,4,8,128]{4,3,2,1,0:T(8,128)(2,1)} copy(bf16[1,64,4,8,128]{4,3,2,1,0:T(8,128)(2,1)S(1)} %shard_map.73) | data formatting | bytes 1048576

commit v5 on v4

--- a/solution.py
+++ b/solution.py
@@ -149,10 +149,10 @@
                 for x in range(LX):
                     z_all[layer, side, x] = e_all[side, x].astype(BF)
 
-    def launch(layer, *stages):
+    def launch(layer, *stages, first=lambda entry: 0):
         for stage in stages:
             pack(layer, stage)
-        for which, entry in enumerate(PLAN):
+        for which, entry in sorted(enumerate(PLAN), key=lambda item: first(item[1])):
             if entry[1] in stages:
                 message(layer, which, a, out_rows, in_rows, send, recv).start()
 
@@ -173,8 +173,7 @@
     for x in inner_planes:
         relay_in(x)
     pl.semaphore_wait(barrier, len(WAYS))
-    for stage in (1, 0, 2, 3):
-        launch(0, stage)
+    launch(0, *range(4), first=lambda entry: (entry[0][2] == 0) + (entry[0][1] == 0 and entry[0][2] == 0))
 
     none = jnp.zeros((C, C), BF)
     for layer in range(3):

time: 33.8 us -> 33.7 us (level)
  no operation moved by 1% of the time
where the time goes in v5:
time: 33.7 us; the launch traced here: 33.6 us
  Pallas kernels  32.8 us (97%)
  local copies, waits for them, and re-layouts  0.8 us (2%)
    pallas_call x1, Pallas kernels, shards(): pl.pallas_call(kernel, out_shape=jax.ShapeDtypeStruct(field.shape, BF), i...  32.8 us
    unnamed x1, local copies, waits for them, and re-layouts  0.8 us

profile of v5, /device:TPU:1, one launch (start us, length us, event | category | flops | bytes accessed | tf_op | source)
XLA Modules:
  0.0 33.6 jit_solution(15419538374030904386)
XLA Ops:
  0.0 32.8 %shard_map.73 = bf16[1,64,4,8,128]{4,3,2,1,0:T(8,128)(2,1)S(1)} custom-call(bf16[1,64,4,8,128]{4,3,2,1,0:T(8,128)(2,1)} %field.1, bf16[3,3,3,64,64]{4,3,2,1,0:T(8,128)(2,1)} %k_one.1, bf16[3,3,3,64,64]{4,3,2,1,0:T(8,128)(2,1)} %k_two.1, bf16[3,3,3,64,64]{4,3,2,1,0:T(8,128)(2,1)} %k_three.1, f32[1,64]{1,0:T(1,128)} %bitcast.3, f32[1,64]{1,0:T(1,128)} %bitcast.4, ...), custom_call_target="tpu_custom_call" | custom-call | tf_op jit(solution)/shard_map/pallas_call | solution.py:363
  32.8 0.8 %copy.9 = bf16[1,64,4,8,128]{4,3,2,1,0:T(8,128)(2,1)} copy(bf16[1,64,4,8,128]{4,3,2,1,0:T(8,128)(2,1)S(1)} %shard_map.73) | data formatting | bytes 1048576

commit v6 on v5

--- a/solution.py
+++ b/solution.py
@@ -25,8 +25,8 @@
     entries = [((0, dy, 0), 0, (2, LX - 2)) for dy in both]
     entries += [((dx, dy, dz), 1, None) for dx in both for dy in both for dz in both]
     entries += [((0, dy, dz), 1, None) for dy in both for dz in both]
+    entries += [((0, dy, 0), 1, piece) for dy in both for piece in ((1, 1), (LX, 1))]
     entries += [((dx, dy, 0), 1, None) for dx in both for dy in both]
-    entries += [((0, dy, 0), 1, piece) for dy in both for piece in ((1, 1), (LX, 1))]
     entries += [((dx, 0, 0), 1, (1, 2)) for dx in both]
     entries += [((dx, 0, dz), 2, None) for dx in both for dz in both]
     entries += [((0, 0, dz), 2, None) for dz in both]

time: 33.7 us -> 33.7 us (level)
  no operation moved by 1% of the time
where the time goes in v6:
time: 33.7 us; the launch traced here: 33.6 us
  Pallas kernels  32.8 us (97%)
  local copies, waits for them, and re-layouts  0.8 us (2%)
    pallas_call x1, Pallas kernels, shards(): pl.pallas_call(kernel, out_shape=jax.ShapeDtypeStruct(field.shape, BF), i...  32.8 us
    unnamed x1, local copies, waits for them, and re-layouts  0.8 us

profile of v6, /device:TPU:1, one launch (start us, length us, event | category | flops | bytes accessed | tf_op | source)
XLA Modules:
  0.0 33.6 jit_solution(9878293023463294027)
XLA Ops:
  0.0 32.8 %shard_map.73 = bf16[1,64,4,8,128]{4,3,2,1,0:T(8,128)(2,1)S(1)} custom-call(bf16[1,64,4,8,128]{4,3,2,1,0:T(8,128)(2,1)} %field.1, bf16[3,3,3,64,64]{4,3,2,1,0:T(8,128)(2,1)} %k_one.1, bf16[3,3,3,64,64]{4,3,2,1,0:T(8,128)(2,1)} %k_two.1, bf16[3,3,3,64,64]{4,3,2,1,0:T(8,128)(2,1)} %k_three.1, f32[1,64]{1,0:T(1,128)} %bitcast.3, f32[1,64]{1,0:T(1,128)} %bitcast.4, ...), custom_call_target="tpu_custom_call" | custom-call | tf_op jit(solution)/shard_map/pallas_call | solution.py:363
  32.8 0.8 %copy.9 = bf16[1,64,4,8,128]{4,3,2,1,0:T(8,128)(2,1)} copy(bf16[1,64,4,8,128]{4,3,2,1,0:T(8,128)(2,1)S(1)} %shard_map.73) | data formatting | bytes 1048576
